TPU v7x, 32 devices: a whole 2x2x4 slice. The times are simulated.
32 devices in a mesh: seq: 8 (over y, x, core), fsdp: 4 (over z).
Axes of the slice: x: 2, y: 2, z: 4, core: 2. Of those that a mesh axis runs over, the one named last changes fastest.
Arguments:
- hidden: bfloat16 [4096, 8192], P(('seq', 'fsdp')), may hold values from -6 to 6
- kv_blocks: bfloat16 [8192, 1024], P('fsdp'), may hold values from -0.0625 to 0.0625
- kv_scale: float32 [64, 8], P('fsdp'), may hold values from 0.5 to 2
- queries: bfloat16 [4096, 4096], P(('seq', 'fsdp')), may hold values from -24 to 24
- grad_out: bfloat16 [4096, 4096], P(('seq', 'fsdp')), may hold values from -6 to 6
Outputs:
- attn_out: bfloat16 [4096, 4096], P(('seq', 'fsdp'))
- grad_queries: bfloat16 [4096, 4096], P(('seq', 'fsdp'))
- grad_hidden: bfloat16 [4096, 8192], P(('seq', 'fsdp'))
- weight_grad: float32 [8192, 1024], P('fsdp')
All inputs are finite; a program needn't handle non-finite values.
Results may differ from a plain program's by a relative error of at most 0.0075.
The roundings to bfloat16 on the way count: a program that leaves them out, or rounds other values in their place, can miss the bound.
Values may be sent and summed in bfloat16 or wider, within the bound.
A program may use at most 128 MiB of HBM per device.

v0:
```python
import jax
import jax.numpy as jnp
from jax import lax
from jax.sharding import PartitionSpec as P

HEADS = 32
KV_HEADS = 4
HEAD = 128
QB = 128


NEG = -1e30


def shifted(block, axis, distance):
    devices = range(lax.axis_size(axis))
    route = [(i - distance, i) for i in devices if i - distance in devices]
    return lax.ppermute(block, axis, route)


def dequantize(blocks, scale):
    rows, cols = blocks.shape
    grid = blocks.astype(jnp.float32).reshape(scale.shape[0], QB, scale.shape[1], QB)
    return (grid * scale[:, None, :, None]).reshape(rows, cols).astype(jnp.bfloat16)


def attend_group(operands, allowed):
    qgrp, kgrp, vgrp, ggrp = operands
    factor = 1.0 / float(HEAD) ** 0.5
    scores = jnp.einsum("rhd,kd->rhk", qgrp, kgrp, preferred_element_type=jnp.float32) * factor
    scores = jnp.where(allowed[:, None, :], scores, NEG)
    top = jnp.max(scores, axis=-1, keepdims=True)
    expd = jnp.exp(scores - top)
    probs = expd / jnp.sum(expd, axis=-1, keepdims=True)
    probs_b = probs.astype(jnp.bfloat16)
    output = jnp.einsum("rhk,kd->rhd", probs_b, vgrp, preferred_element_type=jnp.float32).astype(
        jnp.bfloat16
    )
    dprobs = jnp.einsum("rhd,kd->rhk", ggrp, vgrp, preferred_element_type=jnp.float32)
    delta = jnp.sum(probs * dprobs, axis=-1, keepdims=True)
    dscores = (probs * (dprobs - delta) * factor).astype(jnp.bfloat16)
    gradq = jnp.einsum("rhk,kd->rhd", dscores, kgrp, preferred_element_type=jnp.float32).astype(
        jnp.bfloat16
    )
    gradk = jnp.einsum("rhk,rhd->kd", dscores, qgrp, preferred_element_type=jnp.float32)
    gradv = jnp.einsum("rhk,rhd->kd", probs_b, ggrp, preferred_element_type=jnp.float32)
    return (output, gradq, gradk, gradv)


def attend(queries, window, grad_out, allowed):
    rows = queries.shape[0]
    count = window.shape[0]
    group = HEADS // KV_HEADS
    kvw = KV_HEADS * HEAD
    qgrp = queries.reshape(rows, KV_HEADS, group, HEAD).transpose(1, 0, 2, 3)
    ggrp = grad_out.reshape(rows, KV_HEADS, group, HEAD).transpose(1, 0, 2, 3)
    kgrp = window[:, :kvw].reshape(count, KV_HEADS, HEAD).transpose(1, 0, 2)
    vgrp = window[:, kvw:].reshape(count, KV_HEADS, HEAD).transpose(1, 0, 2)
    output, gradq, gradk, gradv = lax.map(
        lambda ops: attend_group(ops, allowed), (qgrp, kgrp, vgrp, ggrp)
    )
    output = output.transpose(1, 0, 2, 3).reshape(rows, HEADS * HEAD)
    gradq = gradq.transpose(1, 0, 2, 3).reshape(rows, HEADS * HEAD)
    gradk = gradk.transpose(1, 0, 2).reshape(count, kvw)
    gradv = gradv.transpose(1, 0, 2).reshape(count, kvw)
    return (output, gradq, jnp.concatenate([gradk, gradv], axis=1))


def body(hidden, kv_blocks, kv_scale, queries, grad_out):
    tok = hidden.shape[0]
    groups = lax.axis_size("fsdp")
    reach = groups // 2
    place = lax.axis_index("fsdp")
    linear = lax.axis_index("seq") * groups + place
    weights = dequantize(kv_blocks, kv_scale)
    columns = lax.all_to_all(hidden, "fsdp", split_axis=1, concat_axis=0, tiled=True)
    rows = columns
    kv = lax.psum_scatter(
        jnp.dot(rows, weights, preferred_element_type=jnp.float32),
        "fsdp",
        scatter_dimension=0,
        tiled=True,
    ).astype(jnp.bfloat16)
    pieces = []
    for offset in range(reach, 0, -1):
        pieces.append(shifted(kv, ("seq", "fsdp"), offset))
    window = jnp.concatenate(pieces + [kv], axis=0)
    base = linear * tok
    qpos = base + jnp.arange(tok, dtype=jnp.int32)
    kpos = base - reach * tok + jnp.arange((reach + 1) * tok, dtype=jnp.int32)
    span = reach * tok
    allowed = (
        (qpos[:, None] - kpos[None, :] < span)
        & (kpos[None, :] <= qpos[:, None])
        & (kpos[None, :] >= 0)
    )
    attn_out, grad_queries, dwin = attend(queries, window, grad_out, allowed)
    total = dwin[reach * tok :]
    inside = total
    for offset in range(1, reach + 1):
        piece = dwin[(reach - offset) * tok : (reach - offset + 1) * tok]
        returned = shifted(piece, ("seq", "fsdp"), -offset)
        total = total + returned
        inside = inside + jnp.where(place + offset < groups, returned, jnp.zeros_like(returned))
    all_grad = total.astype(jnp.bfloat16)
    seg_grad = inside.astype(jnp.bfloat16)
    spread = lax.dot_general(
        lax.all_gather(seg_grad, "fsdp", axis=0, tiled=True),
        weights,
        (((1,), (1,)), ((), ())),
        preferred_element_type=jnp.float32,
    ).astype(jnp.bfloat16)
    grad_hidden = lax.all_to_all(spread, "fsdp", split_axis=0, concat_axis=1, tiled=True)
    rows = columns
    shard_grad = lax.dot_general(
        rows,
        lax.all_gather(all_grad, "fsdp", axis=0, tiled=True),
        (((0,), (0,)), ((), ())),
        preferred_element_type=jnp.float32,
    )
    weight_grad = lax.psum(shard_grad, "seq")
    return (attn_out, grad_queries, grad_hidden, weight_grad)


def solution(mesh):
    return jax.shard_map(
        body,
        mesh=mesh,
        in_specs=(
            P(("seq", "fsdp"), None),
            P("fsdp", None),
            P("fsdp", None),
            P(("seq", "fsdp"), None),
            P(("seq", "fsdp"), None),
        ),
        out_specs=(
            P(("seq", "fsdp"), None),
            P(("seq", "fsdp"), None),
            P(("seq", "fsdp"), None),
            P("fsdp", None),
        ),
        check_vma=False,
    )
```

profile of v0, /device:TPU:27, one launch (start us, length us, event | category | flops | bytes accessed | tf_op | source)
XLA Modules:
  0.0 501.2 jit_solution(12745964746301407682)
XLA Ops:
  11.2 4.7 all-to-all-start
  16.0 45.2 %all-to-all-done = bf16[128,4,2048]{0,2,1:T(8,128)(2,1)S(1)} async-done(((bf16[128,4,2048]{0,2,1:T(8,128)(2,1)}), bf16[128,4,2048]{0,2,1:T(8,128)(2,1)S(1)}, u32[]{:S(2)}, u32[]{:S(2)}) %all-to-all-start) | async-done | bytes 2097184 | tf_op jit(solution)/shard_map/all_to_all | solution.py:76
  73.8 43.9 %reduce-scatter.2.cloned.1.call-done = f32[128,1024]{0,1:T(8,128)} async-done(((f32[512,1024]{0,1:T(8,128)}), f32[128,1024]{0,1:T(8,128)}) %reduce-scatter.2.cloned.1.call-update) | async-done | bytes 524304 | tf_op jit(solution)/shard_map/reduce_scatter | solution.py:78
  118.7 5.5 %collective-permute-start.1 = (bf16[128,1024]{0,1:T(8,128)(2,1)S(1)}, bf16[128,1024]{0,1:T(8,128)(2,1)S(1)}, u32[]{:S(2)}, u32[]{:S(2)}) collective-permute-start(bf16[128,1024]{0,1:T(8,128)(2,1)S(1)} %convert_element_type.32), channel_id=1, source_target_pairs={{0,1},{1,2},{2,3},{3,4},{4,5},{5,6},{6,7},{7,8},{8,9},{9,10},{10,1... | collective-permute-start | bytes 786440 | tf_op jit(solution)/shard_map/ppermute | solution.py:18
  130.4 9.8 %collective-permute-done = bf16[128,1024]{0,1:T(8,128)(2,1)} collective-permute-done((bf16[128,1024]{0,1:T(8,128)(2,1)S(1)}, bf16[128,1024]{0,1:T(8,128)(2,1)}, u32[]{:S(2)}, u32[]{:S(2)}) %collective-permute-start) | collective-permute-done | bytes 262176 | tf_op jit(solution)/shard_map/ppermute | solution.py:18
  141.7 110.8 %while.17 = (s32[]{:T(128)}, bf16[4,128,8,128]{3,1,2,0:T(8,128)(2,1)}, bf16[4,128,8,128]{3,1,2,0:T(8,128)(2,1)}, f32[4,384,128]{1,2,0:T(8,128)S(1)}, f32[4,384,1...) while((s32[]{:T(128)}, ...), condition=%wide.region_5.6_spmd.clone, body=%wide.region_1.5_spmd.clone.sunk | while | flops 816830336 | bytes 25336436 | solution.py:59
  149.9 8.0 %fusion.155 = bf16[4,128,8,128]{3,1,2,0:T(8,128)(2,1)} fusion(bf16[4,128,8,128]{3,1,2,0:T(8,128)(2,1)} %get-tuple-element.254, s32[]{:T(128)S(6)} %copy.76, f32[128,8,384]{2,0,1:T(8,128)S(1)} %fusion.154, bf16[4,384,128]{2,1,0:T(8,128)(2,1)} %copy-done.9, f32[128,8,384]{2,0,1:T(8,128)} %get-tuple-element.238, f32[128,8]{0,1:T(8,128)S(1)} %get-tuple-element.237), kind=kOutput, calls=%fused_computation.16.clone.1 | convolution fusion | flops 103548288 | bytes 6661120 | tf_op jit(solution)/shard_map/while/body/eval_jaxpr/rhk,kd->rhd/dot_general | solution.py:42
  157.9 7.5 %fusion.156 = f32[4,384,128]{1,2,0:T(8,128)S(1)} fusion(f32[4,384,128]{1,2,0:T(8,128)S(1)} %get-tuple-element.255, s32[]{:T(128)S(6)} %copy.76, f32[128,8,384]{2,0,1:T(8,128)S(1)} %fusion.154, bf16[4,128,8,128]{1,3,2,0:T(8,128)(2,1)} %get-tuple-element.270, f32[128,8,384]{2,0,1:T(8,128)} %get-tuple-element.238, f32[128,8]{0,1:T(8,128)S(1)} %get-tuple-element.237), kind=kOutput, calls=%fused_computation.20.clone.1 | convolution fusion | flops 103417216 | bytes 6759424 | tf_op jit(solution)/shard_map/while/body/eval_jaxpr/rhk,rhd->kd/dot_general | solution.py:45
  177.6 8.0 %fusion.155 = bf16[4,128,8,128]{3,1,2,0:T(8,128)(2,1)} fusion(bf16[4,128,8,128]{3,1,2,0:T(8,128)(2,1)} %get-tuple-element.254, s32[]{:T(128)S(6)} %copy.76, f32[128,8,384]{2,0,1:T(8,128)S(1)} %fusion.154, bf16[4,384,128]{2,1,0:T(8,128)(2,1)} %copy-done.9, f32[128,8,384]{2,0,1:T(8,128)} %get-tuple-element.238, f32[128,8]{0,1:T(8,128)S(1)} %get-tuple-element.237), kind=kOutput, calls=%fused_computation.16.clone.1 | convolution fusion | flops 103548288 | bytes 6661120 | tf_op jit(solution)/shard_map/while/body/eval_jaxpr/rhk,kd->rhd/dot_general | solution.py:42
  185.6 7.5 %fusion.156 = f32[4,384,128]{1,2,0:T(8,128)S(1)} fusion(f32[4,384,128]{1,2,0:T(8,128)S(1)} %get-tuple-element.255, s32[]{:T(128)S(6)} %copy.76, f32[128,8,384]{2,0,1:T(8,128)S(1)} %fusion.154, bf16[4,128,8,128]{1,3,2,0:T(8,128)(2,1)} %get-tuple-element.270, f32[128,8,384]{2,0,1:T(8,128)} %get-tuple-element.238, f32[128,8]{0,1:T(8,128)S(1)} %get-tuple-element.237), kind=kOutput, calls=%fused_computation.20.clone.1 | convolution fusion | flops 103417216 | bytes 6759424 | tf_op jit(solution)/shard_map/while/body/eval_jaxpr/rhk,rhd->kd/dot_general | solution.py:45
  205.3 8.0 %fusion.155 = bf16[4,128,8,128]{3,1,2,0:T(8,128)(2,1)} fusion(bf16[4,128,8,128]{3,1,2,0:T(8,128)(2,1)} %get-tuple-element.254, s32[]{:T(128)S(6)} %copy.76, f32[128,8,384]{2,0,1:T(8,128)S(1)} %fusion.154, bf16[4,384,128]{2,1,0:T(8,128)(2,1)} %copy-done.9, f32[128,8,384]{2,0,1:T(8,128)} %get-tuple-element.238, f32[128,8]{0,1:T(8,128)S(1)} %get-tuple-element.237), kind=kOutput, calls=%fused_computation.16.clone.1 | convolution fusion | flops 103548288 | bytes 6661120 | tf_op jit(solution)/shard_map/while/body/eval_jaxpr/rhk,kd->rhd/dot_general | solution.py:42
  213.3 7.5 %fusion.156 = f32[4,384,128]{1,2,0:T(8,128)S(1)} fusion(f32[4,384,128]{1,2,0:T(8,128)S(1)} %get-tuple-element.255, s32[]{:T(128)S(6)} %copy.76, f32[128,8,384]{2,0,1:T(8,128)S(1)} %fusion.154, bf16[4,128,8,128]{1,3,2,0:T(8,128)(2,1)} %get-tuple-element.270, f32[128,8,384]{2,0,1:T(8,128)} %get-tuple-element.238, f32[128,8]{0,1:T(8,128)S(1)} %get-tuple-element.237), kind=kOutput, calls=%fused_computation.20.clone.1 | convolution fusion | flops 103417216 | bytes 6759424 | tf_op jit(solution)/shard_map/while/body/eval_jaxpr/rhk,rhd->kd/dot_general | solution.py:45
  233.0 8.0 %fusion.155 = bf16[4,128,8,128]{3,1,2,0:T(8,128)(2,1)} fusion(bf16[4,128,8,128]{3,1,2,0:T(8,128)(2,1)} %get-tuple-element.254, s32[]{:T(128)S(6)} %copy.76, f32[128,8,384]{2,0,1:T(8,128)S(1)} %fusion.154, bf16[4,384,128]{2,1,0:T(8,128)(2,1)} %copy-done.9, f32[128,8,384]{2,0,1:T(8,128)} %get-tuple-element.238, f32[128,8]{0,1:T(8,128)S(1)} %get-tuple-element.237), kind=kOutput, calls=%fused_computation.16.clone.1 | convolution fusion | flops 103548288 | bytes 6661120 | tf_op jit(solution)/shard_map/while/body/eval_jaxpr/rhk,kd->rhd/dot_general | solution.py:42
  241.0 7.5 %fusion.156 = f32[4,384,128]{1,2,0:T(8,128)S(1)} fusion(f32[4,384,128]{1,2,0:T(8,128)S(1)} %get-tuple-element.255, s32[]{:T(128)S(6)} %copy.76, f32[128,8,384]{2,0,1:T(8,128)S(1)} %fusion.154, bf16[4,128,8,128]{1,3,2,0:T(8,128)(2,1)} %get-tuple-element.270, f32[128,8,384]{2,0,1:T(8,128)} %get-tuple-element.238, f32[128,8]{0,1:T(8,128)S(1)} %get-tuple-element.237), kind=kOutput, calls=%fused_computation.20.clone.1 | convolution fusion | flops 103417216 | bytes 6759424 | tf_op jit(solution)/shard_map/while/body/eval_jaxpr/rhk,rhd->kd/dot_general | solution.py:45
  256.4 6.4 %collective-permute-start.2 = (f32[128,1024]{0,1:T(8,128)S(1)}, f32[128,1024]{0,1:T(8,128)}, u32[]{:S(2)}, u32[]{:S(2)}) collective-permute-start(f32[128,1024]{0,1:T(8,128)S(1)} %get-tuple-element.156), channel_id=1, source_target_pairs={{1,0},{2,1},{3,2},{4,3},{5,4},{6,5},{7,6},{8,7},{9,8},{10,9},{11,1... | collective-permute-start | bytes 1572872 | tf_op jit(solution)/shard_map/ppermute | solution.py:18
  262.7 33.3 %collective-permute-done.3 = f32[128,1024]{0,1:T(8,128)} collective-permute-done((f32[128,1024]{0,1:T(8,128)}, f32[128,1024]{0,1:T(8,128)}, u32[]{:S(2)}, u32[]{:S(2)}) %collective-permute-start.3) | collective-permute-done | bytes 524320 | tf_op jit(solution)/shard_map/ppermute | solution.py:18
  299.4 25.6 %all-gather.5.cloned.1.call-done = bf16[512,1024]{0,1:T(8,128)(2,1)} async-done(((bf16[128,1024]{0,1:T(8,128)(2,1)}), bf16[512,1024]{0,1:T(8,128)(2,1)}) %all-gather.5.cloned.1.call-update) | async-done | bytes 1048592 | tf_op jit(solution)/shard_map/all_gather | solution.py:117
  325.0 6.8 %convolution_bitcast_fusion.1 = f32[2048,1024]{0,1:T(8,128)} fusion(bf16[512,1024]{0,1:T(8,128)(2,1)} %all-gather.5.cloned.1.call-done, bf16[512,2048]{1,0:T(8,128)(2,1)S(1)} %bitcast.162), kind=kOutput, calls=%fused_computation.64 | convolution fusion | flops 2147483648 | bytes 11534336 | tf_op jit(solution)/shard_map/dot_general | solution.py:115
  331.8 23.0 %all-gather.3.cloned.1.call-done = bf16[512,1024]{0,1:T(8,128)(2,1)} async-done(((bf16[128,1024]{0,1:T(8,128)(2,1)}), bf16[512,1024]{0,1:T(8,128)(2,1)}) %all-gather.3.cloned.1.call-update) | async-done | bytes 1048592 | tf_op jit(solution)/shard_map/all_gather | solution.py:108
  354.8 9.0 %convolution_convert_fusion.1 = bf16[512,2048]{1,0:T(8,128)(2,1)} fusion(bf16[512,1024]{0,1:T(8,128)(2,1)} %all-gather.3.cloned.1.call-done, f32[256,8,8,128]{3,2,1,0:T(8,128)} %bitcast.157, bf16[2048,1024]{1,0:T(8,128)(2,1)} %param.8), kind=kOutput, calls=%fused_computation.65 | convolution fusion | flops 2154823680 | bytes 15728640 | tf_op jit(solution)/shard_map/dot_general | solution.py:107
  363.8 6.2 %all-to-all-start.1 = ((bf16[4,128,2048]{2,1,0:T(8,128)(2,1)}), bf16[4,128,2048]{2,1,0:T(8,128)(2,1)S(1)}, u32[]{:S(2)}, u32[]{:S(2)}) async-start(bf16[4,128,2048]{2,1,0:T(8,128)(2,1)} %bitcast.18), calls=%async_computation.2 | async-start | bytes 4194304 | tf_op jit(solution)/shard_map/all_to_all | solution.py:113
  374.2 41.4 %all-to-all-done.1 = bf16[4,128,2048]{2,1,0:T(8,128)(2,1)S(1)} async-done(((bf16[4,128,2048]{2,1,0:T(8,128)(2,1)}), bf16[4,128,2048]{2,1,0:T(8,128)(2,1)S(1)}, u32[]{:S(2)}, u32[]{:S(2)}) %all-to-all-start.1) | async-done | bytes 2097184 | tf_op jit(solution)/shard_map/all_to_all | solution.py:113
  417.0 68.4 %all-reduce.2.cloned.1.call-done = f32[2048,1024]{0,1:T(8,128)} async-done(((f32[2048,1024]{0,1:T(8,128)}), f32[2048,1024]{0,1:T(8,128)}) %all-reduce.2.cloned.1.call-update) | async-done | bytes 8388624 | tf_op jit(solution)/shard_map/psum | solution.py:121
  485.4 9.2 %copy.49 = f32[2048,1024]{1,0:T(8,128)} copy(f32[2048,1024]{0,1:T(8,128)} %all-reduce.2.cloned.1.call-done) | data formatting | bytes 16777216
  (105 shorter events, 86.8 us)
Async XLA Ops:
  11.2 4.7 copy-start.11
  11.2 49.9 %all-to-all-start = ((bf16[128,4,2048]{0,2,1:T(8,128)(2,1)}), bf16[128,4,2048]{0,2,1:T(8,128)(2,1)S(1)}, u32[]{:S(2)}, u32[]{:S(2)}) async-start(bf16[128,4,2048]{0,2,1:T(8,128)(2,1)} %bitcast.160), calls=%async_computation | async-start | bytes 4194304 | tf_op jit(solution)/shard_map/all_to_all | solution.py:76
  15.9 101.8 %reduce-scatter.2.cloned.1.call-start = ((), (), s32[]{:S(2)}) async-start(), calls=%async_computation.3 | async-start | bytes 2621440 | tf_op jit(solution)/shard_map/reduce_scatter | solution.py:78
  63.7 4.9 copy-start.1
  63.7 5.9 %copy-start.2 = (bf16[4,128,2048]{2,1,0:T(8,128)(2,1)S(1)}, bf16[4,128,2048]{2,1,0:T(8,128)(2,1)}, u32[]{:S(2)}) copy-start(bf16[4,128,2048]{2,1,0:T(8,128)(2,1)} %copy.38) | copy-start | bytes 6291460
  73.7 53.4 %copy-start.6 = (bf16[128,4096]{1,0:T(8,128)(2,1)S(1)}, bf16[128,4096]{1,0:T(8,128)(2,1)}, u32[]{:S(2)}) copy-start(bf16[128,4096]{1,0:T(8,128)(2,1)} %param.10) | copy-start | bytes 3145732
  73.7 251.3 %all-gather.5.cloned.1.call-start = ((), (), s32[]{:S(2)}) async-start(), calls=%async_computation.5 | async-start | bytes 1310720 | tf_op jit(solution)/shard_map/all_gather | solution.py:117
  118.7 11.6 %collective-permute-start.1 = (bf16[128,1024]{0,1:T(8,128)(2,1)S(1)}, bf16[128,1024]{0,1:T(8,128)(2,1)S(1)}, u32[]{:S(2)}, u32[]{:S(2)}) collective-permute-start(bf16[128,1024]{0,1:T(8,128)(2,1)S(1)} %convert_element_type.32), channel_id=1, source_target_pairs={{0,1},{1,2},{2,3},{3,4},{4,5},{5,6},{6,7},{7,8},{8,9},{9,10},{10,1... | collective-permute-start | bytes 786440 | tf_op jit(solution)/shard_map/ppermute | solution.py:18
  124.2 15.9 %collective-permute-start = (bf16[128,1024]{0,1:T(8,128)(2,1)S(1)}, bf16[128,1024]{0,1:T(8,128)(2,1)}, u32[]{:S(2)}, u32[]{:S(2)}) collective-permute-start(bf16[128,1024]{0,1:T(8,128)(2,1)S(1)} %convert_element_type.32), channel_id=1, source_target_pairs={{0,2},{1,3},{2,4},{3,5},{4,6},{5,7},{6,8},{7,9},{8,10},{9,11},{10,... | collective-permute-start | bytes 786440 | tf_op jit(solution)/shard_map/ppermute | solution.py:18
  141.8 6.9 %copy-start.4 = (bf16[4,384,128]{2,1,0:T(8,128)(2,1)}, bf16[4,384,128]{2,1,0:T(8,128)(2,1)S(1)}, u32[]{:S(2)}) copy-start(bf16[4,384,128]{2,1,0:T(8,128)(2,1)S(1)} %get-tuple-element.272) | copy-start | bytes 1179652 | tf_op jit(solution)/shard_map/while
  141.8 6.9 %copy-start.9 = (bf16[4,384,128]{2,1,0:T(8,128)(2,1)}, bf16[4,384,128]{2,1,0:T(8,128)(2,1)S(1)}, u32[]{:S(2)}) copy-start(bf16[4,384,128]{2,1,0:T(8,128)(2,1)S(1)} %get-tuple-element.271) | copy-start | bytes 1179652 | tf_op jit(solution)/shard_map/while
  169.4 6.9 %copy-start.4 = (bf16[4,384,128]{2,1,0:T(8,128)(2,1)}, bf16[4,384,128]{2,1,0:T(8,128)(2,1)S(1)}, u32[]{:S(2)}) copy-start(bf16[4,384,128]{2,1,0:T(8,128)(2,1)S(1)} %get-tuple-element.272) | copy-start | bytes 1179652 | tf_op jit(solution)/shard_map/while
  169.4 6.9 %copy-start.9 = (bf16[4,384,128]{2,1,0:T(8,128)(2,1)}, bf16[4,384,128]{2,1,0:T(8,128)(2,1)S(1)}, u32[]{:S(2)}) copy-start(bf16[4,384,128]{2,1,0:T(8,128)(2,1)S(1)} %get-tuple-element.271) | copy-start | bytes 1179652 | tf_op jit(solution)/shard_map/while
  197.1 6.9 %copy-start.4 = (bf16[4,384,128]{2,1,0:T(8,128)(2,1)}, bf16[4,384,128]{2,1,0:T(8,128)(2,1)S(1)}, u32[]{:S(2)}) copy-start(bf16[4,384,128]{2,1,0:T(8,128)(2,1)S(1)} %get-tuple-element.272) | copy-start | bytes 1179652 | tf_op jit(solution)/shard_map/while
  197.1 6.9 %copy-start.9 = (bf16[4,384,128]{2,1,0:T(8,128)(2,1)}, bf16[4,384,128]{2,1,0:T(8,128)(2,1)S(1)}, u32[]{:S(2)}) copy-start(bf16[4,384,128]{2,1,0:T(8,128)(2,1)S(1)} %get-tuple-element.271) | copy-start | bytes 1179652 | tf_op jit(solution)/shard_map/while
  224.8 6.9 %copy-start.4 = (bf16[4,384,128]{2,1,0:T(8,128)(2,1)}, bf16[4,384,128]{2,1,0:T(8,128)(2,1)S(1)}, u32[]{:S(2)}) copy-start(bf16[4,384,128]{2,1,0:T(8,128)(2,1)S(1)} %get-tuple-element.272) | copy-start | bytes 1179652 | tf_op jit(solution)/shard_map/while
  224.8 6.9 %copy-start.9 = (bf16[4,384,128]{2,1,0:T(8,128)(2,1)}, bf16[4,384,128]{2,1,0:T(8,128)(2,1)S(1)}, u32[]{:S(2)}) copy-start(bf16[4,384,128]{2,1,0:T(8,128)(2,1)S(1)} %get-tuple-element.271) | copy-start | bytes 1179652 | tf_op jit(solution)/shard_map/while
  254.4 41.6 %collective-permute-start.3 = (f32[128,1024]{0,1:T(8,128)}, f32[128,1024]{0,1:T(8,128)}, u32[]{:S(2)}, u32[]{:S(2)}) collective-permute-start(f32[128,1024]{0,1:T(8,128)} %get-tuple-element.157), channel_id=1, source_target_pairs={{2,0},{3,1},{4,2},{5,3},{6,4},{7,5},{8,6},{9,7},{10,8},{11,9},{12,... | collective-permute-start | bytes 1572872 | tf_op jit(solution)/shard_map/ppermute | solution.py:18
  256.4 39.7 %collective-permute-start.2 = (f32[128,1024]{0,1:T(8,128)S(1)}, f32[128,1024]{0,1:T(8,128)}, u32[]{:S(2)}, u32[]{:S(2)}) collective-permute-start(f32[128,1024]{0,1:T(8,128)S(1)} %get-tuple-element.156), channel_id=1, source_target_pairs={{1,0},{2,1},{3,2},{4,3},{5,4},{6,5},{7,6},{8,7},{9,8},{10,9},{11,1... | collective-permute-start | bytes 1572872 | tf_op jit(solution)/shard_map/ppermute | solution.py:18
  262.7 62.2 %copy-start.3 = (bf16[4,128,2048]{2,1,0:T(8,128)(2,1)S(1)}, bf16[4,128,2048]{2,1,0:T(8,128)(2,1)}, u32[]{:S(2)}) copy-start(bf16[4,128,2048]{2,1,0:T(8,128)(2,1)} %copy.38) | copy-start | bytes 6291460
  298.4 56.4 %all-gather.3.cloned.1.call-start = ((), (), s32[]{:S(2)}) async-start(), calls=%async_computation.4 | async-start | bytes 1310720 | tf_op jit(solution)/shard_map/all_gather | solution.py:108
  299.1 186.3 %all-reduce.2.cloned.1.call-start = ((), (), s32[]{:S(2)}) async-start(), calls=%async_computation.6 | async-start | bytes 16777216 | tf_op jit(solution)/shard_map/psum | solution.py:121
  363.8 6.2 %copy-start.8 = (bf16[4,128,8,128]{3,1,2,0:T(8,128)(2,1)S(1)}, bf16[4,128,8,128]{3,1,2,0:T(8,128)(2,1)}, u32[]{:S(2)}) copy-start(bf16[4,128,8,128]{3,1,2,0:T(8,128)(2,1)} %get-tuple-element.60) | copy-start | bytes 3145732
  363.8 51.8 %all-to-all-start.1 = ((bf16[4,128,2048]{2,1,0:T(8,128)(2,1)}), bf16[4,128,2048]{2,1,0:T(8,128)(2,1)S(1)}, u32[]{:S(2)}, u32[]{:S(2)}) async-start(bf16[4,128,2048]{2,1,0:T(8,128)(2,1)} %bitcast.18), calls=%async_computation.2 | async-start | bytes 4194304 | tf_op jit(solution)/shard_map/all_to_all | solution.py:113
  (10 other events, 37.5 us)
Sparse Core Ops, SparseCore 0:
  73.8 43.8 reduce-scatter.1
  298.5 26.3 all-gather.4
  326.5 28.2 all-gather.2
  358.1 127.2 all-reduce.1
where the time goes:
time: 504 us; the launch traced here: 501 us
  waiting for transfers between devices  292 us (58%)
  matrix products  130 us (26%)
  local copies, waits for them, and re-layouts  31 us (6%)
  starting transfers between devices  27.8 us (6%)
  between operations  13.9 us (3%)
  other arithmetic  6.92 us (1%)
    psum x1, waiting for transfers between devices, body(): weight_grad = lax.psum(shard_grad, 'seq')  68.4 us
    all_to_all x1, waiting for transfers between devices, body(): lax.all_to_all(hidden, 'fsdp', split_axis=1, concat_axis=0, tiled=True)  45.2 us
    reduce_scatter x1, waiting for transfers between devices, body(): lax.psum_scatter(jnp.dot(rows, weights, preferred_element_type=jnp.float3...  43.9 us
    ppermute x4, waiting for transfers between devices, shifted(): return lax.ppermute(block, axis, route)  43.3 us
    all_to_all x1, waiting for transfers between devices, body(): lax.all_to_all(spread, 'fsdp', split_axis=0, concat_axis=1, tiled=True)  41.4 us
    dot_general x4, matrix products, attend_group(): jnp.einsum('rhk,kd->rhd', dscores, kgrp, preferred_element_type=jnp.float32)  31.9 us
    dot_general x4, matrix products, attend_group(): jnp.einsum('rhk,rhd->kd', dscores, qgrp, preferred_element_type=jnp.float32)  30 us
    all_gather x1, waiting for transfers between devices, body(): lax.all_gather(all_grad, 'fsdp', axis=0, tiled=True)  25.6 us
  transfers between devices with their start and end apart: 10, of which 9 were waited for; matrix products, arithmetic and copies ran while one was open for 5% of the time, Pallas kernels for 0%

commit v1 on v0

v1 whole, which is shorter than its diff:
```python
import functools

import jax
import jax.numpy as jnp
from jax import lax
from jax.experimental import pallas as pl
from jax.experimental.pallas import tpu as pltpu
from jax.sharding import PartitionSpec as P

HEADS = 32
KV_HEADS = 4
HEAD = 128
QB = 128


NEG = -1e30


def shifted(block, axis, distance):
    devices = range(lax.axis_size(axis))
    route = [(i - distance, i) for i in devices if i - distance in devices]
    return lax.ppermute(block, axis, route)


def dequantize(blocks, scale):
    rows, cols = blocks.shape
    grid = blocks.astype(jnp.float32).reshape(scale.shape[0], QB, scale.shape[1], QB)
    return (grid * scale[:, None, :, None]).reshape(rows, cols).astype(jnp.bfloat16)


def attend_kernel(reach, q_ref, g_ref, k_ref, v_ref, out_ref, dq_ref, dk_ref, dv_ref):
    tok = q_ref.shape[0]
    group = q_ref.shape[1] // HEAD
    count = k_ref.shape[0]
    span = reach * tok
    factor = 1.0 / float(HEAD) ** 0.5
    base = (lax.axis_index("seq") * lax.axis_size("fsdp") + lax.axis_index("fsdp")) * tok
    row = lax.broadcasted_iota(jnp.int32, (tok, count), 0)
    col = lax.broadcasted_iota(jnp.int32, (tok, count), 1)
    allowed = (col > row) & (col <= row + span) & (col >= span - base)
    keys = k_ref[...]
    values = v_ref[...]
    nt = (((1,), (1,)), ((), ()))
    tn = (((0,), (0,)), ((), ()))
    ps, ds, qs, gs = [], [], [], []
    for h in range(group):
        cut = slice(h * HEAD, (h + 1) * HEAD)
        q = q_ref[:, cut]
        g = g_ref[:, cut]
        scores = lax.dot_general(q, keys, nt, preferred_element_type=jnp.float32) * factor
        scores = jnp.where(allowed, scores, NEG)
        expd = jnp.exp(scores - jnp.max(scores, axis=-1, keepdims=True))
        probs = expd * (1.0 / jnp.sum(expd, axis=-1, keepdims=True))
        probs_b = probs.astype(jnp.bfloat16)
        out_ref[:, cut] = jnp.dot(probs_b, values, preferred_element_type=jnp.float32).astype(jnp.bfloat16)
        dprobs = lax.dot_general(g, values, nt, preferred_element_type=jnp.float32)
        delta = jnp.sum(probs * dprobs, axis=-1, keepdims=True)
        dscores = (probs * (dprobs - delta) * factor).astype(jnp.bfloat16)
        dq_ref[:, cut] = jnp.dot(dscores, keys, preferred_element_type=jnp.float32).astype(jnp.bfloat16)
        ps.append(probs_b)
        ds.append(dscores)
        qs.append(q)
        gs.append(g)
    cat = lambda parts: jnp.concatenate(parts, axis=0)
    dk_ref[...] = lax.dot_general(cat(ds), cat(qs), tn, preferred_element_type=jnp.float32)
    dv_ref[...] = lax.dot_general(cat(ps), cat(gs), tn, preferred_element_type=jnp.float32)


def attend(queries, window, grad_out, reach):
    tok, width = queries.shape
    count = window.shape[0]
    heads = window.shape[1] // (2 * HEAD)
    wide = pl.BlockSpec((tok, width // heads), lambda i: (0, i))
    key = pl.BlockSpec((count, HEAD), lambda i: (0, i))
    value = pl.BlockSpec((count, HEAD), lambda i: (0, i + heads))
    out, dq, dk, dv = pl.pallas_call(
        functools.partial(attend_kernel, reach),
        grid=(heads,),
        in_specs=[wide, wide, key, value],
        out_specs=[wide, wide, key, key],
        out_shape=[
            jax.ShapeDtypeStruct((tok, width), jnp.bfloat16),
            jax.ShapeDtypeStruct((tok, width), jnp.bfloat16),
            jax.ShapeDtypeStruct((count, heads * HEAD), jnp.float32),
            jax.ShapeDtypeStruct((count, heads * HEAD), jnp.float32),
        ],
        cost_estimate=pl.CostEstimate(flops=12 * tok * width * count, bytes_accessed=8 * tok * width, transcendentals=0),
        name="attend",
    )(queries, grad_out, window, window)
    return out, dq, jnp.concatenate([dk, dv], axis=1)


def body(hidden, kv_blocks, kv_scale, queries, grad_out):
    tok = hidden.shape[0]
    groups = lax.axis_size("fsdp")
    reach = groups // 2
    place = lax.axis_index("fsdp")
    linear = lax.axis_index("seq") * groups + place
    weights = dequantize(kv_blocks, kv_scale)
    columns = lax.all_to_all(hidden, "fsdp", split_axis=1, concat_axis=0, tiled=True)
    rows = columns
    kv = lax.psum_scatter(
        jnp.dot(rows, weights, preferred_element_type=jnp.float32),
        "fsdp",
        scatter_dimension=0,
        tiled=True,
    ).astype(jnp.bfloat16)
    pieces = []
    for offset in range(reach, 0, -1):
        pieces.append(shifted(kv, ("seq", "fsdp"), offset))
    window = jnp.concatenate(pieces + [kv], axis=0)
    attn_out, grad_queries, dwin = attend(queries, window, grad_out, reach)
    total = dwin[reach * tok :]
    inside = total
    for offset in range(1, reach + 1):
        piece = dwin[(reach - offset) * tok : (reach - offset + 1) * tok]
        returned = shifted(piece, ("seq", "fsdp"), -offset)
        total = total + returned
        inside = inside + jnp.where(place + offset < groups, returned, jnp.zeros_like(returned))
    all_grad = total.astype(jnp.bfloat16)
    seg_grad = inside.astype(jnp.bfloat16)
    spread = lax.dot_general(
        lax.all_gather(seg_grad, "fsdp", axis=0, tiled=True),
        weights,
        (((1,), (1,)), ((), ())),
        preferred_element_type=jnp.float32,
    ).astype(jnp.bfloat16)
    grad_hidden = lax.all_to_all(spread, "fsdp", split_axis=0, concat_axis=1, tiled=True)
    rows = columns
    shard_grad = lax.dot_general(
        rows,
        lax.all_gather(all_grad, "fsdp", axis=0, tiled=True),
        (((0,), (0,)), ((), ())),
        preferred_element_type=jnp.float32,
    )
    weight_grad = lax.psum(shard_grad.astype(jnp.bfloat16), "seq").astype(jnp.float32)
    return (attn_out, grad_queries, grad_hidden, weight_grad)


def solution(mesh):
    return jax.shard_map(
        body,
        mesh=mesh,
        in_specs=(
            P(("seq", "fsdp"), None),
            P("fsdp", None),
            P("fsdp", None),
            P(("seq", "fsdp"), None),
            P(("seq", "fsdp"), None),
        ),
        out_specs=(
            P(("seq", "fsdp"), None),
            P(("seq", "fsdp"), None),
            P(("seq", "fsdp"), None),
            P("fsdp", None),
        ),
        check_vma=False,
    )
```

time: 504 us -> 388 us (0.77)
  matrix products: 130 us -> 19.2 us
  Pallas kernels: 0 us -> 23.1 us
  waiting for transfers between devices: 292 us -> 277 us
  local copies, waits for them, and re-layouts: 31 us -> 23.2 us
    dot_general x20 -> x0, matrix products: 98.2 us -> none  [the longest x4 31.9 us: attend_group(): jnp.einsum('rhk,kd->rhd', dscores, kgrp, preferred_element_type=jnp.float32)]
    all_to_all x1, waiting for transfers between devices: 41.4 us -> 0.01 us  [body(): lax.all_to_all(spread, 'fsdp', split_axis=0, concat_axis=1, tiled=True)]
    pallas_call x0 -> x1, Pallas kernels: none -> 23.1 us  [attend(): pl.pallas_call(functools.partial(attend_kernel, reach), grid=(heads,), in...]
    psum x1, waiting for transfers between devices: 68.4 us -> 87.5 us  [body(): lax.psum(shard_grad.astype(jnp.bfloat16), 'seq').astype(jnp.float32)]
    sub x4 -> x0, matrix products: 11.8 us -> none  [attend_group(): expd = jnp.exp(scores - top)]
    unnamed x21 -> x14, local copies, waits for them, and re-layouts: 22.1 us -> 17.6 us
  transfers between devices with their start and end apart: 10 -> 10, of which waited for: 9 -> 9; matrix products, arithmetic and copies ran while one was open for 5% -> 6% of each run, Pallas kernels for 0% -> 0%
where the time goes in v1:
time: 388 us; the launch traced here: 385 us
  waiting for transfers between devices  277 us (71%)
  starting transfers between devices  25.9 us (7%)
  local copies, waits for them, and re-layouts  23.2 us (6%)
  Pallas kernels  23.1 us (6%)
  matrix products  19.2 us (5%)
  between operations  13.8 us (4%)
    psum x1, waiting for transfers between devices, body(): lax.psum(shard_grad.astype(jnp.bfloat16), 'seq').astype(jnp.float32)  87.5 us
    ppermute x4, waiting for transfers between devices, shifted(): return lax.ppermute(block, axis, route)  47.3 us
    all_to_all x1, waiting for transfers between devices, body(): lax.all_to_all(hidden, 'fsdp', split_axis=1, concat_axis=0, tiled=True)  45.2 us
    reduce_scatter x1, waiting for transfers between devices, body(): lax.psum_scatter(jnp.dot(rows, weights, preferred_element_type=jnp.float3...  43.9 us
    all_gather x1, waiting for transfers between devices, body(): lax.all_gather(all_grad, 'fsdp', axis=0, tiled=True)  26.3 us
    all_gather x1, waiting for transfers between devices, body(): lax.all_gather(seg_grad, 'fsdp', axis=0, tiled=True)  25.8 us
    pallas_call x1, Pallas kernels, attend(): pl.pallas_call(functools.partial(attend_kernel, reach), grid=(heads,), in...  23.1 us
    unnamed x14, local copies, waits for them, and re-layouts  17.6 us
  transfers between devices with their start and end apart: 10, of which 9 were waited for; matrix products, arithmetic and copies ran while one was open for 6% of the time, Pallas kernels for 0%

profile of v1, /device:TPU:27, one launch (start us, length us, event | category | flops | bytes accessed | tf_op | source)
XLA Modules:
  0.0 385.0 jit_solution(15753351379655463794)
XLA Ops:
  7.2 4.1 %copy.18 = bf16[128,8192]{0,1:T(8,128)(2,1)} copy(bf16[128,8192]{1,0:T(8,128)(2,1)} %param.5) | data formatting | bytes 4194304 | tf_op args[0]
  11.2 4.7 %all-to-all-start = ((bf16[128,4,2048]{0,2,1:T(8,128)(2,1)}), bf16[128,4,2048]{0,2,1:T(8,128)(2,1)S(1)}, u32[]{:S(2)}, u32[]{:S(2)}) async-start(bf16[128,4,2048]{0,2,1:T(8,128)(2,1)} %bitcast.27), calls=%async_computation | async-start | bytes 4194304 | tf_op jit(solution)/shard_map/all_to_all | solution.py:100
  16.0 45.2 %all-to-all-done = bf16[128,4,2048]{0,2,1:T(8,128)(2,1)S(1)} async-done(((bf16[128,4,2048]{0,2,1:T(8,128)(2,1)}), bf16[128,4,2048]{0,2,1:T(8,128)(2,1)S(1)}, u32[]{:S(2)}, u32[]{:S(2)}) %all-to-all-start) | async-done | bytes 2097184 | tf_op jit(solution)/shard_map/all_to_all | solution.py:100
  61.2 2.6 copy.19
  64.4 4.2 %copy-done = f32[16,128,8,128]{3,2,1,0:T(8,128)} copy-done((f32[16,128,8,128]{3,2,1,0:T(8,128)}, f32[16,128,8,128]{3,2,1,0:T(8,128)S(1)}, u32[]{:S(2)}) %copy-start) | copy-done | bytes 8388632
  69.6 4.0 %convolution_bitcast_fusion = f32[512,1024]{1,0:T(8,128)} fusion(bf16[512,2048]{1,0:T(8,128)(2,1)S(1)} %bitcast.29, f32[256,8,8,128]{3,2,1,0:T(8,128)S(1)} %bitcast.23, bf16[2048,1024]{1,0:T(8,128)(2,1)S(1)} %copy-done.1), kind=kOutput, calls=%fused_computation.4 | convolution fusion | flops 2153775104 | bytes 16777216 | tf_op jit(solution)/shard_map/dot_general | solution.py:103
  73.7 43.9 %reduce-scatter.2.cloned.1.call-done = f32[128,1024]{1,0:T(8,128)} async-done(((f32[512,1024]{1,0:T(8,128)}), f32[128,1024]{1,0:T(8,128)}) %reduce-scatter.2.cloned.1.call-update) | async-done | bytes 524304 | tf_op jit(solution)/shard_map/reduce_scatter | solution.py:102
  118.7 5.5 %collective-permute-start.1 = (bf16[128,1024]{1,0:T(8,128)(2,1)S(1)}, bf16[128,1024]{1,0:T(8,128)(2,1)S(1)}, u32[]{:S(2)}, u32[]{:S(2)}) collective-permute-start(bf16[128,1024]{1,0:T(8,128)(2,1)S(1)} %convert_element_type.29), channel_id=1, source_target_pairs={{0,1},{1,2},{2,3},{3,4},{4,5},{5,6},{6,7},{7,8},{8,9},{9,10},{10,1... | collective-permute-start | bytes 786440 | tf_op jit(solution)/shard_map/ppermute | solution.py:22
  124.2 2.6 collective-permute-start
  126.8 3.5 collective-permute-done.1
  130.3 9.6 %collective-permute-done = bf16[128,1024]{1,0:T(8,128)(2,1)S(1)} collective-permute-done((bf16[128,1024]{1,0:T(8,128)(2,1)S(1)}, bf16[128,1024]{1,0:T(8,128)(2,1)S(1)}, u32[]{:S(2)}, u32[]{:S(2)}) %collective-permute-start) | collective-permute-done | bytes 262176 | tf_op jit(solution)/shard_map/ppermute | solution.py:22
  140.9 23.1 %attend.1 = (bf16[128,4096]{1,0:T(8,128)(2,1)}, bf16[128,4096]{1,0:T(8,128)(2,1)}, f32[384,512]{1,0:T(8,128)}, f32[384,512]{1,0:T(8,128)}) custom-call(bf16[128,4096]{1,0:T(8,128)(2,1)} %q_ref.1, bf16[128,4096]{1,0:T(8,128)(2,1)} %g_ref.1, bf16[384,1024]{1,0:T(8,128)(2,1)} %pad_maximum_fusion.k_ref.v_ref, bf16[384,1024]{1,0:T(8,128)(2,1)} %pad_maximum_fusion.k_ref.v_ref), custom_call_target="tpu_custom_call" | custom-call | flops 2415919104 | bytes 4194304 | tf_op jit(solution)/shard_map/attend/pallas_call | solution.py:76
  166.4 3.5 collective-permute-start.2
  169.8 4.8 %collective-permute-start.3 = (f32[128,1024]{1,0:T(8,128)S(1)}, f32[128,1024]{1,0:T(8,128)S(1)}, u32[]{:S(2)}, u32[]{:S(2)}) collective-permute-start(f32[128,1024]{1,0:T(8,128)S(1)} %get-tuple-element.27), channel_id=1, source_target_pairs={{2,0},{3,1},{4,2},{5,3},{6,4},{7,5},{8,6},{9,7},{10,8},{11,9},{12,... | collective-permute-start | bytes 1572872 | tf_op jit(solution)/shard_map/ppermute | solution.py:22
  174.7 12.7 %collective-permute-done.2 = f32[128,1024]{1,0:T(8,128)S(1)} collective-permute-done((f32[128,1024]{1,0:T(8,128)}, f32[128,1024]{1,0:T(8,128)S(1)}, u32[]{:S(2)}, u32[]{:S(2)}) %collective-permute-start.2) | collective-permute-done | bytes 524320 | tf_op jit(solution)/shard_map/ppermute | solution.py:22
  187.4 21.4 %collective-permute-done.3 = f32[128,1024]{1,0:T(8,128)S(1)} collective-permute-done((f32[128,1024]{1,0:T(8,128)S(1)}, f32[128,1024]{1,0:T(8,128)S(1)}, u32[]{:S(2)}, u32[]{:S(2)}) %collective-permute-start.3) | collective-permute-done | bytes 524320 | tf_op jit(solution)/shard_map/ppermute | solution.py:22
  210.5 25.8 %all-gather.3.cloned.1.call-done = bf16[512,1024]{1,0:T(8,128)(2,1)} async-done(((bf16[128,1024]{1,0:T(8,128)(2,1)}), bf16[512,1024]{1,0:T(8,128)(2,1)}) %all-gather.3.cloned.1.call-update) | async-done | bytes 1048592 | tf_op jit(solution)/shard_map/all_gather | solution.py:123
  236.4 8.9 %convolution_convert_fusion = bf16[512,2048]{1,0:T(8,128)(2,1)} fusion(bf16[512,1024]{1,0:T(8,128)(2,1)} %all-gather.3.cloned.1.call-done, f32[256,8,8,128]{3,2,1,0:T(8,128)} %bitcast.24, bf16[2048,1024]{1,0:T(8,128)(2,1)} %param.6), kind=kOutput, calls=%fused_computation.3 | convolution fusion | flops 2154823680 | bytes 15728640 | tf_op jit(solution)/shard_map/dot_general | solution.py:122
  245.3 4.8 %all-to-all-start.1 = ((bf16[4,128,2048]{2,1,0:T(8,128)(2,1)}), bf16[4,128,2048]{2,1,0:T(8,128)(2,1)S(1)}, u32[]{:S(2)}, u32[]{:S(2)}) async-start(bf16[4,128,2048]{2,1,0:T(8,128)(2,1)} %bitcast.4), calls=%async_computation.2 | async-start | bytes 4194304 | tf_op jit(solution)/shard_map/all_to_all | solution.py:128
  250.1 26.3 %all-gather.5.cloned.1.call-done = bf16[512,1024]{1,0:T(8,128)(2,1)} async-done(((bf16[128,1024]{1,0:T(8,128)(2,1)}), bf16[512,1024]{1,0:T(8,128)(2,1)}) %all-gather.5.cloned.1.call-update) | async-done | bytes 1048592 | tf_op jit(solution)/shard_map/all_gather | solution.py:132
  276.3 6.3 %convert_bitcast_fusion = bf16[2048,1024]{0,1:T(8,128)(2,1)} fusion(bf16[512,1024]{1,0:T(8,128)(2,1)} %all-gather.5.cloned.1.call-done, bf16[512,2048]{1,0:T(8,128)(2,1)} %bitcast.28), kind=kOutput, calls=%fused_computation.2 | convolution fusion | flops 2149580800 | bytes 7340032 | tf_op jit(solution)/shard_map/dot_general | solution.py:130
  282.7 87.5 %all-reduce.2.cloned.1.call-done = bf16[2048,1024]{0,1:T(8,128)(2,1)} async-done(((bf16[2048,1024]{0,1:T(8,128)(2,1)}), bf16[2048,1024]{0,1:T(8,128)(2,1)}) %all-reduce.2.cloned.1.call-update) | async-done | bytes 4194320 | tf_op jit(solution)/shard_map/psum | solution.py:136
  370.2 6.9 %copy.22 = f32[2048,1024]{1,0:T(8,128)} copy(bf16[2048,1024]{0,1:T(8,128)(2,1)} %all-reduce.2.cloned.1.call-done) | data formatting | bytes 12582912
  377.1 1.5 copy.24
  (26 shorter events, 7.8 us)
Async XLA Ops:
  11.2 4.7 %copy-start.4 = (f32[16,8]{0,1:T(8,128)S(1)}, f32[16,8]{0,1:T(8,128)}, u32[]{:S(2)}) copy-start(f32[16,8]{0,1:T(8,128)} %param.7) | copy-start | bytes 1540
  11.2 49.9 %all-to-all-start = ((bf16[128,4,2048]{0,2,1:T(8,128)(2,1)}), bf16[128,4,2048]{0,2,1:T(8,128)(2,1)S(1)}, u32[]{:S(2)}, u32[]{:S(2)}) async-start(bf16[128,4,2048]{0,2,1:T(8,128)(2,1)} %bitcast.27), calls=%async_computation | async-start | bytes 4194304 | tf_op jit(solution)/shard_map/all_to_all | solution.py:100
  15.9 101.7 %reduce-scatter.2.cloned.1.call-start = ((), (), s32[]{:S(2)}) async-start(), calls=%async_computation.3 | async-start | bytes 2621440 | tf_op jit(solution)/shard_map/reduce_scatter | solution.py:102
  63.7 4.9 %copy-start.1 = (bf16[2048,1024]{1,0:T(8,128)(2,1)S(1)}, bf16[2048,1024]{1,0:T(8,128)(2,1)}, u32[]{:S(2)}) copy-start(bf16[2048,1024]{1,0:T(8,128)(2,1)} %param.6) | copy-start | bytes 12582916
  63.7 5.9 %copy-start.2 = (bf16[4,128,2048]{2,1,0:T(8,128)(2,1)S(1)}, bf16[4,128,2048]{2,1,0:T(8,128)(2,1)}, u32[]{:S(2)}) copy-start(bf16[4,128,2048]{2,1,0:T(8,128)(2,1)} %copy.19) | copy-start | bytes 6291460
  64.4 4.3 %copy-start = (f32[16,128,8,128]{3,2,1,0:T(8,128)}, f32[16,128,8,128]{3,2,1,0:T(8,128)S(1)}, u32[]{:S(2)}) copy-start(f32[16,128,8,128]{3,2,1,0:T(8,128)S(1)} %mul.11) | copy-start | bytes 25165828
  73.6 162.7 %all-gather.3.cloned.1.call-start = ((), (), s32[]{:S(2)}) async-start(), calls=%async_computation.4 | async-start | bytes 1310720 | tf_op jit(solution)/shard_map/all_gather | solution.py:123
  118.7 11.6 %collective-permute-start.1 = (bf16[128,1024]{1,0:T(8,128)(2,1)S(1)}, bf16[128,1024]{1,0:T(8,128)(2,1)S(1)}, u32[]{:S(2)}, u32[]{:S(2)}) collective-permute-start(bf16[128,1024]{1,0:T(8,128)(2,1)S(1)} %convert_element_type.29), channel_id=1, source_target_pairs={{0,1},{1,2},{2,3},{3,4},{4,5},{5,6},{6,7},{7,8},{8,9},{9,10},{10,1... | collective-permute-start | bytes 786440 | tf_op jit(solution)/shard_map/ppermute | solution.py:22
  124.2 15.8 %collective-permute-start = (bf16[128,1024]{1,0:T(8,128)(2,1)S(1)}, bf16[128,1024]{1,0:T(8,128)(2,1)S(1)}, u32[]{:S(2)}, u32[]{:S(2)}) collective-permute-start(bf16[128,1024]{1,0:T(8,128)(2,1)S(1)} %convert_element_type.29), channel_id=1, source_target_pairs={{0,2},{1,3},{2,4},{3,5},{4,6},{5,7},{6,8},{7,9},{8,10},{9,11},{10,... | collective-permute-start | bytes 786440 | tf_op jit(solution)/shard_map/ppermute | solution.py:22
  164.0 1.4 copy-start.3
  166.4 21.0 %collective-permute-start.2 = (f32[128,1024]{1,0:T(8,128)}, f32[128,1024]{1,0:T(8,128)S(1)}, u32[]{:S(2)}, u32[]{:S(2)}) collective-permute-start(f32[128,1024]{1,0:T(8,128)} %get-tuple-element.26), channel_id=1, source_target_pairs={{1,0},{2,1},{3,2},{4,3},{5,4},{6,5},{7,6},{8,7},{9,8},{10,9},{11,1... | collective-permute-start | bytes 1572872 | tf_op jit(solution)/shard_map/ppermute | solution.py:22
  169.8 39.0 %collective-permute-start.3 = (f32[128,1024]{1,0:T(8,128)S(1)}, f32[128,1024]{1,0:T(8,128)S(1)}, u32[]{:S(2)}, u32[]{:S(2)}) collective-permute-start(f32[128,1024]{1,0:T(8,128)S(1)} %get-tuple-element.27), channel_id=1, source_target_pairs={{2,0},{3,1},{4,2},{5,3},{6,4},{7,5},{8,6},{9,7},{10,8},{11,9},{12,... | collective-permute-start | bytes 1572872 | tf_op jit(solution)/shard_map/ppermute | solution.py:22
  209.8 66.5 %all-gather.5.cloned.1.call-start = ((), (), s32[]{:S(2)}) async-start(), calls=%async_computation.5 | async-start | bytes 1310720 | tf_op jit(solution)/shard_map/all_gather | solution.py:132
  245.3 131.8 %all-to-all-start.1 = ((bf16[4,128,2048]{2,1,0:T(8,128)(2,1)}), bf16[4,128,2048]{2,1,0:T(8,128)(2,1)S(1)}, u32[]{:S(2)}, u32[]{:S(2)}) async-start(bf16[4,128,2048]{2,1,0:T(8,128)(2,1)} %bitcast.4), calls=%async_computation.2 | async-start | bytes 4194304 | tf_op jit(solution)/shard_map/all_to_all | solution.py:128
  250.1 120.1 %all-reduce.2.cloned.1.call-start = ((), (), s32[]{:S(2)}) async-start(), calls=%async_computation.6 | async-start | bytes 8388608 | tf_op jit(solution)/shard_map/psum | solution.py:136
Sparse Core Ops, SparseCore 0:
  73.7 43.8 reduce-scatter.1
  209.9 26.4 all-gather.2
  237.9 38.3 all-gather.4
  282.8 87.3 all-reduce.1

commit v2 on v1

--- a/solution.py
+++ b/solution.py
@@ -20,12 +20,6 @@
     devices = range(lax.axis_size(axis))
     route = [(i - distance, i) for i in devices if i - distance in devices]
     return lax.ppermute(block, axis, route)
-
-
-def dequantize(blocks, scale):
-    rows, cols = blocks.shape
-    grid = blocks.astype(jnp.float32).reshape(scale.shape[0], QB, scale.shape[1], QB)
-    return (grid * scale[:, None, :, None]).reshape(rows, cols).astype(jnp.bfloat16)
 
 
 def attend_kernel(reach, q_ref, g_ref, k_ref, v_ref, out_ref, dq_ref, dk_ref, dv_ref):
@@ -90,51 +84,423 @@
     return out, dq, jnp.concatenate([dk, dv], axis=1)
 
 
+def flipped(index, mask):
+    for place in range(mask.bit_length()):
+        if mask >> place & 1:
+            index = index + (1 << place) * (1 - 2 * (index // (1 << place) % 2))
+    return index
+
+
+def orders_of(bits):
+    return (list(range(1, bits)) + [0], list(range(bits - 1, 0, -1)) + [0])
+
+
+def project_kernel(seqs, groups, hid_ref, blk_ref, sc_ref, w_ref, kv_ref, acc, zsend, zrecv, qsend, qrecv):
+    s = lax.axis_index("seq")
+    z = lax.axis_index("fsdp")
+    rows = blk_ref.shape[0]
+    unit = rows // seqs
+    half = unit // 2
+    bits = seqs.bit_length() - 1
+    chunk = min(512, rows)
+
+    def scale_block(i, carry):
+        at = pl.multiple_of(i * QB, QB)
+        block = blk_ref[pl.ds(at, QB), :].astype(jnp.float32) * sc_ref[pl.ds(i, 1), :]
+        w_ref[pl.ds(pl.multiple_of(z * rows + at, QB), QB), :] = block.astype(jnp.bfloat16)
+        return carry
+
+    lax.fori_loop(0, rows // QB, scale_block, 0)
+
+    def line_copy(shard, up):
+        piece = w_ref.at[pl.ds(pl.multiple_of(shard * rows + s * unit, 16), unit), :]
+        return pltpu.make_async_remote_copy(
+            src_ref=piece,
+            dst_ref=piece,
+            send_sem=zsend.at[up, shard],
+            recv_sem=zrecv.at[shard],
+            device_id=(s, z + 1 if up else z - 1),
+            device_id_type=pl.DeviceIdType.MESH,
+        )
+
+    def cube_copy(turn, shard, order, step, which, incoming):
+        bit = order[step]
+        mask = 0
+        for k in range(step):
+            if which >> k & 1:
+                mask |= 1 << order[k]
+        h = 0 if order is orders[0] else 1
+        owner = flipped(s, mask | (1 << bit) if incoming else mask)
+        piece = w_ref.at[pl.ds(pl.multiple_of(shard * rows + owner * unit + h * half, 16), half), :]
+        slot = (1 << step) - 1 + which
+        return pltpu.make_async_remote_copy(
+            src_ref=piece,
+            dst_ref=piece,
+            send_sem=qsend.at[turn, h, slot],
+            recv_sem=qrecv.at[turn, h, slot],
+            device_id=(flipped(s, 1 << bit), z),
+            device_id_type=pl.DeviceIdType.MESH,
+        )
+
+    orders = orders_of(bits)
+    near = jnp.minimum(z, groups - 1 - z)
+
+    def shard_at(turn):
+        step = turn // 2 + 1
+        paired = z - step if turn % 2 == 0 else z + step
+        far = turn - near + 1
+        single = jnp.where(z > groups - 1 - z, z - far, z + far)
+        return jnp.where(turn < 2 * near, paired, single)
+
+    shards = [shard_at(turn) for turn in range(groups - 1)]
+
+    @pl.when(z < groups - 1)
+    def _():
+        line_copy(z, 1).start()
+
+    @pl.when(z > 0)
+    def _():
+        line_copy(z, 0).start()
+
+    acc[...] = jnp.zeros_like(acc)
+
+    def multiply(shard):
+        def part(i, carry):
+            at = pl.multiple_of(shard * rows + i * chunk, 128)
+            acc[...] += jnp.dot(
+                hid_ref[:, pl.ds(at, chunk)], w_ref[pl.ds(at, chunk), :], preferred_element_type=jnp.float32
+            )
+            return carry
+
+        lax.fori_loop(0, rows // chunk, part, 0)
+
+    multiply(z)
+    for tick in range(groups - 1 + bits):
+        for stage in range(bits, -1, -1):
+            turn = tick - stage
+            if turn < 0 or turn >= groups - 1:
+                continue
+            shard = shards[turn]
+            if stage == 0:
+                line_copy(shard, 0).wait_recv()
+
+                @pl.when((shard < z) & (z < groups - 1))
+                def _():
+                    line_copy(shard, 1).start()
+
+                @pl.when((shard > z) & (z > 0))
+                def _():
+                    line_copy(shard, 0).start()
+            else:
+                for order in orders:
+                    for which in range(1 << (stage - 1)):
+                        cube_copy(turn, shard, order, stage - 1, which, True).wait_recv()
+            if stage < bits:
+                for order in orders:
+                    for which in range(1 << stage):
+                        cube_copy(turn, shard, order, stage, which, False).start()
+            else:
+                multiply(shard)
+    kv_ref[...] = acc[...].astype(jnp.bfloat16)
+    for shard in range(groups):
+
+        @pl.when((shard <= z) & (z < groups - 1))
+        def _():
+            line_copy(shard, 1).wait_send()
+
+        @pl.when((shard >= z) & (z > 0))
+        def _():
+            line_copy(shard, 0).wait_send()
+
+    for turn in range(groups - 1):
+        for order in orders:
+            for stage in range(bits):
+                for which in range(1 << stage):
+                    cube_copy(turn, shards[turn], order, stage, which, False).wait_send()
+
+
+def project(hidden, kv_blocks, kv_scale):
+    seqs = lax.axis_size("seq")
+    groups = lax.axis_size("fsdp")
+    tok, width = hidden.shape
+    cols = kv_blocks.shape[1]
+    spread = jnp.repeat(kv_scale, QB, axis=1)
+    vmem = pl.BlockSpec(memory_space=pltpu.VMEM)
+    return pl.pallas_call(
+        functools.partial(project_kernel, seqs, groups),
+        out_shape=[
+            jax.ShapeDtypeStruct((width, cols), jnp.bfloat16),
+            jax.ShapeDtypeStruct((tok, cols), jnp.bfloat16),
+        ],
+        in_specs=[vmem] * 3,
+        out_specs=[vmem] * 2,
+        scratch_shapes=[
+            pltpu.VMEM((tok, cols), jnp.float32),
+            pltpu.SemaphoreType.DMA((2, groups)),
+            pltpu.SemaphoreType.DMA((groups,)),
+            pltpu.SemaphoreType.DMA((groups - 1, 2, seqs - 1)),
+            pltpu.SemaphoreType.DMA((groups - 1, 2, seqs - 1)),
+        ],
+        compiler_params=pltpu.CompilerParams(has_side_effects=True),
+        name="project",
+    )(hidden, kv_blocks, spread)
+
+
+def finish_kernel(
+    seqs, groups, reach, back_ref, own_ref, w_ref, col_ref, gh_ref, wg_ref,
+    ret, every, inside, acc, sends, recvs, hsend, hrecv, gsend, grecv, rsend, rrecv, asend, arecv,
+):
+    s = lax.axis_index("seq")
+    z = lax.axis_index("fsdp")
+    linear = s * groups + z
+    devices = seqs * groups
+    tok, cols = own_ref.shape
+    rows = col_ref.shape[1]
+    bits = seqs.bit_length() - 1
+    mesh_id = pl.DeviceIdType.MESH
+
+    def halo_copy(offset, incoming):
+        other = linear + offset if incoming else linear - offset
+        return pltpu.make_async_remote_copy(
+            src_ref=back_ref.at[pl.ds((reach - offset) * tok, tok), :],
+            dst_ref=ret.at[offset - 1],
+            send_sem=hsend.at[offset - 1],
+            recv_sem=hrecv.at[offset - 1],
+            device_id=(other // groups, other % groups),
+            device_id_type=mesh_id,
+        )
+
+    for offset in range(1, reach + 1):
+
+        @pl.when(linear >= offset)
+        def _():
+            halo_copy(offset, False).start()
+
+    for offset in range(1, reach + 1):
+
+        @pl.when(linear + offset < devices)
+        def _():
+            halo_copy(offset, True).wait_recv()
+
+        @pl.when(linear + offset >= devices)
+        def _():
+            ret[offset - 1] = jnp.zeros((tok, cols), jnp.bfloat16)
+
+    total = own_ref[...]
+    seg = total
+    for offset in range(1, reach + 1):
+        piece = ret[offset - 1].astype(jnp.float32)
+        total = total + piece
+        seg = seg + piece * jnp.where(z + offset < groups, 1.0, 0.0)
+    every[z] = total.astype(jnp.bfloat16)
+    inside[...] = seg.astype(jnp.bfloat16)
+
+    def gather_copy(gap, incoming):
+        other = (z - gap + groups) % groups if incoming else (z + gap) % groups
+        block = every.at[other if incoming else z]
+        return pltpu.make_async_remote_copy(
+            src_ref=block,
+            dst_ref=block,
+            send_sem=gsend.at[gap - 1],
+            recv_sem=grecv.at[gap - 1],
+            device_id=(s, other),
+            device_id_type=mesh_id,
+        )
+
+    for gap in range(1, groups):
+        gather_copy(gap, False).start()
+
+    wide = 512
+
+    def spread(i, carry):
+        at = pl.multiple_of(i * wide, wide)
+        gh_ref[:, pl.ds(at, wide)] = lax.dot_general(
+            inside[...], w_ref[pl.ds(at, wide), :], (((1,), (1,)), ((), ())), preferred_element_type=jnp.float32
+        ).astype(jnp.bfloat16)
+        return carry
+
+    lax.fori_loop(0, w_ref.shape[0] // wide, spread, 0)
+    for gap in range(1, groups):
+        gather_copy(gap, True).wait_recv()
+
+    big = rows // 2
+    tile = min(256, big)
+    low = s % 2
+    sibling = flipped(s, 1)
+    grads = every[...].reshape(groups * tok, cols)
+
+    def product(at):
+        return lax.dot_general(
+            col_ref[:, pl.ds(at, tile)], grads, (((0,), (0,)), ((), ())), preferred_element_type=jnp.float32
+        )
+
+    def theirs(i, carry):
+        at = pl.multiple_of(i * tile, tile)
+        sends[0][pl.ds(at, tile), :] = product(pl.multiple_of((1 - low) * big + at, tile)).astype(jnp.bfloat16)
+        return carry
+
+    lax.fori_loop(0, big // tile, theirs, 0)
+
+    def reduce_copy(step, h, peer):
+        cut = slice(None) if h is None else pl.ds(h * (cols // 2), cols // 2)
+        return pltpu.make_async_remote_copy(
+            src_ref=sends[step].at[:, cut] if h is not None else sends[step],
+            dst_ref=recvs[step].at[:, cut] if h is not None else recvs[step],
+            send_sem=rsend.at[step, h or 0],
+            recv_sem=rrecv.at[step, h or 0],
+            device_id=(peer, z),
+            device_id_type=mesh_id,
+        )
+
+    reduce_copy(0, None, sibling).start()
+
+    def mine(i, carry):
+        at = pl.multiple_of(i * tile, tile)
+        acc[pl.ds(at, tile), :] = product(pl.multiple_of(low * big + at, tile))
+        return carry
+
+    lax.fori_loop(0, big // tile, mine, 0)
+    reduce_copy(0, None, sibling).wait_recv()
+
+    def fold(i, carry):
+        at = pl.multiple_of(i * tile, tile)
+        acc[pl.ds(at, tile), :] += recvs[0][pl.ds(at, tile), :].astype(jnp.float32)
+        return carry
+
+    lax.fori_loop(0, big // tile, fold, 0)
+    orders = (list(range(1, bits)), list(range(bits - 1, 0, -1)))
+    offsets = [[0], [0]]
+    side = cols // 2
+    for step in range(1, bits):
+        size = rows >> (step + 1)
+        for h in range(2):
+            place = orders[h][step - 1]
+            bit = s // (1 << place) % 2
+            start = offsets[h][-1]
+            away = pl.multiple_of(start + (1 - bit) * size, 16)
+            sends[step][:, h * side : (h + 1) * side] = acc[
+                pl.ds(away, size), h * side : (h + 1) * side
+            ].astype(jnp.bfloat16)
+            reduce_copy(step, h, flipped(s, 1 << place)).start()
+            offsets[h].append(start + bit * size)
+        for h in range(2):
+            place = orders[h][step - 1]
+            reduce_copy(step, h, flipped(s, 1 << place)).wait_recv()
+            keep = pl.ds(pl.multiple_of(offsets[h][-1], 16), size)
+            cut = slice(h * side, (h + 1) * side)
+            acc[keep, cut] += recvs[step][:, cut].astype(jnp.float32)
+    size = rows >> bits
+    for h in range(2):
+        at = offsets[h][-1]
+        cut = slice(h * side, (h + 1) * side)
+        wg_ref[pl.ds(pl.multiple_of(low * big + at, 16), size), cut] = acc[
+            pl.ds(pl.multiple_of(at, 16), size), cut
+        ].astype(jnp.bfloat16)
+
+    def spread_copy(step, h, incoming):
+        place = orders[h][step - 1]
+        bit = s // (1 << place) % 2
+        size = rows >> (step + 1)
+        at = low * big + offsets[h][step - 1] + ((1 - bit) if incoming else bit) * size
+        block = wg_ref.at[pl.ds(pl.multiple_of(at, 16), size), pl.ds(h * side, side)]
+        return pltpu.make_async_remote_copy(
+            src_ref=block,
+            dst_ref=block,
+            send_sem=asend.at[step, h],
+            recv_sem=arecv.at[step, h],
+            device_id=(flipped(s, 1 << place), z),
+            device_id_type=mesh_id,
+        )
+
+    for step in range(bits - 1, 0, -1):
+        for h in range(2):
+            spread_copy(step, h, False).start()
+        for h in range(2):
+            spread_copy(step, h, True).wait_recv()
+
+    def last_copy(incoming):
+        block = wg_ref.at[pl.ds(pl.multiple_of(((1 - low) if incoming else low) * big, 16), big), :]
+        return pltpu.make_async_remote_copy(
+            src_ref=block,
+            dst_ref=block,
+            send_sem=asend.at[0, 0],
+            recv_sem=arecv.at[0, 0],
+            device_id=(sibling, z),
+            device_id_type=mesh_id,
+        )
+
+    last_copy(False).start()
+    last_copy(True).wait_recv()
+    for offset in range(1, reach + 1):
+
+        @pl.when(linear >= offset)
+        def _():
+            halo_copy(offset, False).wait_send()
+
+    for gap in range(1, groups):
+        gather_copy(gap, False).wait_send()
+    reduce_copy(0, None, sibling).wait_send()
+    for step in range(1, bits):
+        for h in range(2):
+            reduce_copy(step, h, flipped(s, 1 << orders[h][step - 1])).wait_send()
+            spread_copy(step, h, False).wait_send()
+    last_copy(False).wait_send()
+
+
+def finish(back, own, weights, columns, reach):
+    seqs = lax.axis_size("seq")
+    groups = lax.axis_size("fsdp")
+    tok, cols = own.shape
+    rows = columns.shape[1]
+    bits = seqs.bit_length() - 1
+    vmem = pl.BlockSpec(memory_space=pltpu.VMEM)
+    steps = [pltpu.VMEM((rows >> (k + 1), cols), jnp.bfloat16) for k in range(bits)]
+    dma = pltpu.SemaphoreType.DMA
+    return pl.pallas_call(
+        functools.partial(finish_kernel, seqs, groups, reach),
+        out_shape=[
+            jax.ShapeDtypeStruct((tok, weights.shape[0]), jnp.bfloat16),
+            jax.ShapeDtypeStruct((rows, cols), jnp.bfloat16),
+        ],
+        in_specs=[vmem] * 4,
+        out_specs=[vmem] * 2,
+        scratch_shapes=[
+            pltpu.VMEM((reach, tok, cols), jnp.bfloat16),
+            pltpu.VMEM((groups, tok, cols), jnp.bfloat16),
+            pltpu.VMEM((tok, cols), jnp.bfloat16),
+            pltpu.VMEM((rows // 2, cols), jnp.float32),
+            steps,
+            steps,
+            dma((reach,)),
+            dma((reach,)),
+            dma((groups - 1,)),
+            dma((groups - 1,)),
+            dma((bits, 2)),
+            dma((bits, 2)),
+            dma((bits, 2)),
+            dma((bits, 2)),
+        ],
+        compiler_params=pltpu.CompilerParams(has_side_effects=True),
+        name="finish",
+    )(back, own, weights, columns)
+
+
 def body(hidden, kv_blocks, kv_scale, queries, grad_out):
     tok = hidden.shape[0]
     groups = lax.axis_size("fsdp")
     reach = groups // 2
-    place = lax.axis_index("fsdp")
-    linear = lax.axis_index("seq") * groups + place
-    weights = dequantize(kv_blocks, kv_scale)
-    columns = lax.all_to_all(hidden, "fsdp", split_axis=1, concat_axis=0, tiled=True)
-    rows = columns
-    kv = lax.psum_scatter(
-        jnp.dot(rows, weights, preferred_element_type=jnp.float32),
-        "fsdp",
-        scatter_dimension=0,
-        tiled=True,
-    ).astype(jnp.bfloat16)
+    weights, kv = project(hidden, kv_blocks, kv_scale)
     pieces = []
     for offset in range(reach, 0, -1):
         pieces.append(shifted(kv, ("seq", "fsdp"), offset))
     window = jnp.concatenate(pieces + [kv], axis=0)
+    window, later = lax.optimization_barrier((window, hidden))
+    columns = lax.all_to_all(later, "fsdp", split_axis=1, concat_axis=0, tiled=True)
     attn_out, grad_queries, dwin = attend(queries, window, grad_out, reach)
-    total = dwin[reach * tok :]
-    inside = total
-    for offset in range(1, reach + 1):
-        piece = dwin[(reach - offset) * tok : (reach - offset + 1) * tok]
-        returned = shifted(piece, ("seq", "fsdp"), -offset)
-        total = total + returned
-        inside = inside + jnp.where(place + offset < groups, returned, jnp.zeros_like(returned))
-    all_grad = total.astype(jnp.bfloat16)
-    seg_grad = inside.astype(jnp.bfloat16)
-    spread = lax.dot_general(
-        lax.all_gather(seg_grad, "fsdp", axis=0, tiled=True),
-        weights,
-        (((1,), (1,)), ((), ())),
-        preferred_element_type=jnp.float32,
-    ).astype(jnp.bfloat16)
-    grad_hidden = lax.all_to_all(spread, "fsdp", split_axis=0, concat_axis=1, tiled=True)
-    rows = columns
-    shard_grad = lax.dot_general(
-        rows,
-        lax.all_gather(all_grad, "fsdp", axis=0, tiled=True),
-        (((0,), (0,)), ((), ())),
-        preferred_element_type=jnp.float32,
-    )
-    weight_grad = lax.psum(shard_grad.astype(jnp.bfloat16), "seq").astype(jnp.float32)
-    return (attn_out, grad_queries, grad_hidden, weight_grad)
+    back = dwin[: reach * tok].astype(jnp.bfloat16)
+    own = dwin[reach * tok :]
+    grad_hidden, weight_grad = finish(back, own, weights, columns, reach)
+    return (attn_out, grad_queries, grad_hidden, weight_grad.astype(jnp.float32))
 
 
 def solution(mesh):

time: 388 us -> 289 us (0.74)
  waiting for transfers between devices: 277 us -> 35 us
  Pallas kernels: 23.1 us -> 224 us
  matrix products: 19.2 us -> 0 us
  local copies, waits for them, and re-layouts: 23.2 us -> 8.74 us
  starting transfers between devices: 25.9 us -> 12 us
  between operations: 13.8 us -> 0.7 us
  other arithmetic: 2.97 us -> 8.66 us
    pallas_call x0 -> x2, Pallas kernels: none -> 201 us  [the longest x1 113 us: finish(): pl.pallas_call(functools.partial(finish_kernel, seqs, groups, reach), out...]
    psum x1 -> x0, waiting for transfers between devices: 87.5 us -> none  [body(): lax.psum(shard_grad.astype(jnp.bfloat16), 'seq').astype(jnp.float32)]
    all_gather x2 -> x0, waiting for transfers between devices: 52.1 us -> none  [the longest x1 26.3 us: body(): lax.all_gather(all_grad, 'fsdp', axis=0, tiled=True)]
    reduce_scatter x1 -> x0, waiting for transfers between devices: 43.9 us -> none  [body(): lax.psum_scatter(jnp.dot(rows, weights, preferred_element_type=jnp.float3...]
    ppermute x4 -> x2, waiting for transfers between devices: 47.3 us -> 15.5 us  [shifted(): return lax.ppermute(block, axis, route)]
    all_to_all x2 -> x1, waiting for transfers between devices: 45.2 us -> 19.5 us  [body(): lax.all_to_all(later, 'fsdp', split_axis=1, concat_axis=0, tiled=True)]
    dot_general x3 -> x0, matrix products: 19.2 us -> none  [the longest x1 8.93 us: body(): lax.dot_general(lax.all_gather(seg_grad, 'fsdp', axis=0, tiled=True), wei...]
    unnamed x14 -> x12, local copies, waits for them, and re-layouts: 17.6 us -> 5.42 us
  transfers between devices with their start and end apart: 10 -> 3, of which waited for: 9 -> 3; matrix products, arithmetic and copies ran while one was open for 6% -> 1% of each run, Pallas kernels for 0% -> 8%
where the time goes in v2:
time: 289 us
  Pallas kernels  224 us (78%)
  waiting for transfers between devices  35 us (12%)
  starting transfers between devices  12 us (4%)
  local copies, waits for them, and re-layouts  8.74 us (3%)
  other arithmetic  8.66 us (3%)
    pallas_call x1, Pallas kernels, finish(): pl.pallas_call(functools.partial(finish_kernel, seqs, groups, reach), out...  113 us
    pallas_call x1, Pallas kernels, project(): pl.pallas_call(functools.partial(project_kernel, seqs, groups), out_shape...  88 us
    pallas_call x1, Pallas kernels, attend(): pl.pallas_call(functools.partial(attend_kernel, reach), grid=(heads,), in...  23.1 us
    all_to_all x1, waiting for transfers between devices, body(): lax.all_to_all(later, 'fsdp', split_axis=1, concat_axis=0, tiled=True)  19.5 us
    ppermute x2, waiting for transfers between devices, shifted(): return lax.ppermute(block, axis, route)  15.5 us
    all_to_all x1, starting transfers between devices, body(): lax.all_to_all(later, 'fsdp', split_axis=1, concat_axis=0, tiled=True)  6.96 us
    convert_element_type x1, other arithmetic, body(): weight_grad.astype(jnp.float32)  6.78 us
  transfers between devices with their start and end apart: 3, of which 3 were waited for; matrix products, arithmetic and copies ran while one was open for 1% of the time, Pallas kernels for 8%

profile of v2, /device:TPU:27, one launch (start us, length us, event | category | flops | bytes accessed | tf_op | source)
XLA Modules:
  0.0 289.1 jit_solution(7834648183659826631)
XLA Ops:
  0.6 0.8 copy.9
  1.4 0.1 broadcast_in_dim.3
  1.5 0.7 copy.16
  2.1 88.0 %project.1 = (bf16[8192,1024]{1,0:T(8,128)(2,1)}, bf16[128,1024]{1,0:T(8,128)(2,1)}) custom-call(bf16[128,8192]{1,0:T(8,128)(2,1)} %hid_ref.1, bf16[2048,1024]{1,0:T(8,128)(2,1)} %blk_ref.1, f32[16,1024]{1,0:T(8,128)} %bitcast.14), custom_call_target="tpu_custom_call" | custom-call | tf_op jit(solution)/shard_map/project/pallas_call | solution.py:229
  90.1 2.4 collective-permute-start.1
  92.6 2.6 collective-permute-start
  95.2 4.7 %collective-permute-done.1 = bf16[128,1024]{1,0:T(8,128)(2,1)S(1)} collective-permute-done((bf16[128,1024]{1,0:T(8,128)(2,1)}, bf16[128,1024]{1,0:T(8,128)(2,1)S(1)}, u32[]{:S(2)}, u32[]{:S(2)}) %collective-permute-start.1) | collective-permute-done | bytes 262176 | tf_op jit(solution)/shard_map/ppermute | solution.py:22
  99.9 10.8 %collective-permute-done = bf16[128,1024]{1,0:T(8,128)(2,1)S(1)} collective-permute-done((bf16[128,1024]{1,0:T(8,128)(2,1)}, bf16[128,1024]{1,0:T(8,128)(2,1)S(1)}, u32[]{:S(2)}, u32[]{:S(2)}) %collective-permute-start) | collective-permute-done | bytes 262176 | tf_op jit(solution)/shard_map/ppermute | solution.py:22
  110.7 1.9 pad_maximum_fusion.k_ref.v_ref
  112.6 0.0 copy-done
  112.6 1.5 copy.15
  114.0 7.0 %all-to-all-start = ((bf16[128,4,2048]{2,0,1:T(8,128)(2,1)}), bf16[128,4,2048]{2,0,1:T(8,128)(2,1)S(1)}, u32[]{:S(2)}, u32[]{:S(2)}) async-start(bf16[128,4,2048]{2,0,1:T(8,128)(2,1)} %bitcast.13), calls=%async_computation | async-start | bytes 4194304 | tf_op jit(solution)/shard_map/all_to_all | solution.py:498
  121.0 23.1 %attend.1 = (bf16[128,4096]{1,0:T(8,128)(2,1)}, bf16[128,4096]{1,0:T(8,128)(2,1)}, f32[384,512]{1,0:T(8,128)}, f32[384,512]{1,0:T(8,128)}) custom-call(bf16[128,4096]{1,0:T(8,128)(2,1)} %q_ref.1, bf16[128,4096]{1,0:T(8,128)(2,1)} %g_ref.1, bf16[384,1024]{1,0:T(8,128)(2,1)} %pad_maximum_fusion.k_ref.v_ref, bf16[384,1024]{1,0:T(8,128)(2,1)} %pad_maximum_fusion.k_ref.v_ref), custom_call_target="tpu_custom_call" | custom-call | flops 2415919104 | bytes 4194304 | tf_op jit(solution)/shard_map/attend/pallas_call | solution.py:70
  144.1 1.3 constant_dynamic-update-slice_fusion.1
  145.4 0.1 copy-done.3
  145.5 0.1 constant_dynamic-update-slice_fusion
  145.5 0.9 slice.10.own_ref
  146.4 0.9 slice.12.back_ref
  147.3 19.5 %all-to-all-done = bf16[128,4,2048]{2,0,1:T(8,128)(2,1)S(1)} async-done(((bf16[128,4,2048]{2,0,1:T(8,128)(2,1)}), bf16[128,4,2048]{2,0,1:T(8,128)(2,1)S(1)}, u32[]{:S(2)}, u32[]{:S(2)}) %all-to-all-start) | async-done | bytes 2097184 | tf_op jit(solution)/shard_map/all_to_all | solution.py:498
  166.8 1.3 copy-done.1
  168.1 112.9 %finish.1 = (bf16[128,8192]{1,0:T(8,128)(2,1)}, bf16[2048,1024]{1,0:T(8,128)(2,1)}) custom-call(bf16[256,1024]{1,0:T(8,128)(2,1)} %slice.12.back_ref, f32[128,1024]{1,0:T(8,128)} %slice.10.own_ref, bf16[8192,1024]{1,0:T(8,128)(2,1)} %get-tuple-element.20.w_ref, bf16[512,2048]{1,0:T(8,128)(2,1)} %bitcast.12), custom_call_target="tpu_custom_call" | custom-call | tf_op jit(solution)/shard_map/finish/pallas_call | solution.py:459
  281.0 0.0 copy-start.2
  281.0 6.8 %convert_element_type.4 = f32[2048,1024]{1,0:T(8,128)} convert(bf16[2048,1024]{1,0:T(8,128)(2,1)} %get-tuple-element.23) | non-fusion elementwise | flops 2097152 | bytes 12582912 | tf_op jit(solution)/shard_map/convert_element_type | solution.py:503
  287.8 1.3 copy.19
  (4 shorter events, 0.0 us)
Async XLA Ops:
  2.1 110.4 %copy-start = (bf16[128,8192]{1,0:T(8,128)(2,1)S(1)}, bf16[128,8192]{1,0:T(8,128)(2,1)}, u32[]{:S(2)}) copy-start(bf16[128,8192]{1,0:T(8,128)(2,1)} %hid_ref.1) | copy-start | bytes 6291460
  90.1 9.7 %collective-permute-start.1 = (bf16[128,1024]{1,0:T(8,128)(2,1)}, bf16[128,1024]{1,0:T(8,128)(2,1)S(1)}, u32[]{:S(2)}, u32[]{:S(2)}) collective-permute-start(bf16[128,1024]{1,0:T(8,128)(2,1)} %get-tuple-element.14), channel_id=1, source_target_pairs={{0,1},{1,2},{2,3},{3,4},{4,5},{5,6},{6,7},{7,8},{8,9},{9,10},{10,1... | collective-permute-start | bytes 786440 | tf_op jit(solution)/shard_map/ppermute | solution.py:22
  92.6 18.1 %collective-permute-start = (bf16[128,1024]{1,0:T(8,128)(2,1)}, bf16[128,1024]{1,0:T(8,128)(2,1)S(1)}, u32[]{:S(2)}, u32[]{:S(2)}) collective-permute-start(bf16[128,1024]{1,0:T(8,128)(2,1)} %get-tuple-element.14), channel_id=1, source_target_pairs={{0,2},{1,3},{2,4},{3,5},{4,6},{5,7},{6,8},{7,9},{8,10},{9,11},{10,... | collective-permute-start | bytes 786440 | tf_op jit(solution)/shard_map/ppermute | solution.py:22
  114.0 52.8 %all-to-all-start = ((bf16[128,4,2048]{2,0,1:T(8,128)(2,1)}), bf16[128,4,2048]{2,0,1:T(8,128)(2,1)S(1)}, u32[]{:S(2)}, u32[]{:S(2)}) async-start(bf16[128,4,2048]{2,0,1:T(8,128)(2,1)} %bitcast.13), calls=%async_computation | async-start | bytes 4194304 | tf_op jit(solution)/shard_map/all_to_all | solution.py:498
  144.1 1.4 copy-start.3
  166.8 1.3 copy-start.1
  281.0 6.8 %copy-start.2 = (bf16[128,8192]{1,0:T(8,128)(2,1)S(1)}, bf16[128,8192]{1,0:T(8,128)(2,1)}, u32[]{:S(2)}) copy-start(bf16[128,8192]{1,0:T(8,128)(2,1)} %get-tuple-element.30) | copy-start | bytes 6291460

commit v3 on v2

--- a/solution.py
+++ b/solution.py
@@ -95,7 +95,7 @@
     return (list(range(1, bits)) + [0], list(range(bits - 1, 0, -1)) + [0])
 
 
-def project_kernel(seqs, groups, hid_ref, blk_ref, sc_ref, w_ref, kv_ref, acc, zsend, zrecv, qsend, qrecv):
+def project_kernel(seqs, groups, hid_ref, blk_ref, sc_ref, w_ref, kv_ref, col_ref, acc, zsend, zrecv, qsend, qrecv, csend, crecv):
     s = lax.axis_index("seq")
     z = lax.axis_index("fsdp")
     rows = blk_ref.shape[0]
@@ -112,13 +112,13 @@
 
     lax.fori_loop(0, rows // QB, scale_block, 0)
 
-    def line_copy(shard, up):
-        piece = w_ref.at[pl.ds(pl.multiple_of(shard * rows + s * unit, 16), unit), :]
+    def line_copy(shard, up, h):
+        piece = w_ref.at[pl.ds(pl.multiple_of(shard * rows + s * unit + h * half, 16), half), :]
         return pltpu.make_async_remote_copy(
             src_ref=piece,
             dst_ref=piece,
-            send_sem=zsend.at[up, shard],
-            recv_sem=zrecv.at[shard],
+            send_sem=zsend.at[up, shard, h],
+            recv_sem=zrecv.at[shard, h],
             device_id=(s, z + 1 if up else z - 1),
             device_id_type=pl.DeviceIdType.MESH,
         )
@@ -154,13 +154,27 @@
 
     shards = [shard_at(turn) for turn in range(groups - 1)]
 
-    @pl.when(z < groups - 1)
-    def _():
-        line_copy(z, 1).start()
-
-    @pl.when(z > 0)
-    def _():
-        line_copy(z, 0).start()
+    for h in range(2):
+
+        @pl.when(z < groups - 1)
+        def _():
+            line_copy(z, 1, h).start()
+
+        @pl.when(z > 0)
+        def _():
+            line_copy(z, 0, h).start()
+
+    def column_copy(gap, incoming):
+        other = (z - gap + groups) % groups if incoming else (z + gap) % groups
+        part = pl.multiple_of(other * rows, 128)
+        return pltpu.make_async_remote_copy(
+            src_ref=hid_ref.at[:, pl.ds(part, rows)],
+            dst_ref=col_ref.at[other if incoming else z],
+            send_sem=csend.at[gap - 1],
+            recv_sem=crecv.at[gap - 1],
+            device_id=(s, other),
+            device_id_type=pl.DeviceIdType.MESH,
+        )
 
     acc[...] = jnp.zeros_like(acc)
 
@@ -175,42 +189,50 @@
         lax.fori_loop(0, rows // chunk, part, 0)
 
     multiply(z)
-    for tick in range(groups - 1 + bits):
+    col_ref[z] = hid_ref[:, pl.ds(pl.multiple_of(z * rows, 128), rows)]
+    turns = 2 * (groups - 1)
+    for tick in range(turns + bits):
         for stage in range(bits, -1, -1):
-            turn = tick - stage
-            if turn < 0 or turn >= groups - 1:
+            if not 0 <= tick - stage < turns:
                 continue
+            turn, h = divmod(tick - stage, 2)
+            order = orders[h]
             shard = shards[turn]
             if stage == 0:
-                line_copy(shard, 0).wait_recv()
+                line_copy(shard, 0, h).wait_recv()
 
                 @pl.when((shard < z) & (z < groups - 1))
                 def _():
-                    line_copy(shard, 1).start()
+                    line_copy(shard, 1, h).start()
 
                 @pl.when((shard > z) & (z > 0))
                 def _():
-                    line_copy(shard, 0).start()
+                    line_copy(shard, 0, h).start()
             else:
-                for order in orders:
-                    for which in range(1 << (stage - 1)):
-                        cube_copy(turn, shard, order, stage - 1, which, True).wait_recv()
+                for which in range(1 << (stage - 1)):
+                    cube_copy(turn, shard, order, stage - 1, which, True).wait_recv()
             if stage < bits:
-                for order in orders:
-                    for which in range(1 << stage):
-                        cube_copy(turn, shard, order, stage, which, False).start()
-            else:
+                for which in range(1 << stage):
+                    cube_copy(turn, shard, order, stage, which, False).start()
+            elif h == 1:
                 multiply(shard)
+        if tick == max(turns - 3, 0):
+            for gap in range(1, groups):
+                column_copy(gap, False).start()
     kv_ref[...] = acc[...].astype(jnp.bfloat16)
+    for gap in range(1, groups):
+        column_copy(gap, True).wait_recv()
+        column_copy(gap, False).wait_send()
     for shard in range(groups):
-
-        @pl.when((shard <= z) & (z < groups - 1))
-        def _():
-            line_copy(shard, 1).wait_send()
-
-        @pl.when((shard >= z) & (z > 0))
-        def _():
-            line_copy(shard, 0).wait_send()
+        for h in range(2):
+
+            @pl.when((shard <= z) & (z < groups - 1))
+            def _():
+                line_copy(shard, 1, h).wait_send()
+
+            @pl.when((shard >= z) & (z > 0))
+            def _():
+                line_copy(shard, 0, h).wait_send()
 
     for turn in range(groups - 1):
         for order in orders:
@@ -231,15 +253,18 @@
         out_shape=[
             jax.ShapeDtypeStruct((width, cols), jnp.bfloat16),
             jax.ShapeDtypeStruct((tok, cols), jnp.bfloat16),
+            jax.ShapeDtypeStruct((groups, tok, kv_blocks.shape[0]), jnp.bfloat16),
         ],
         in_specs=[vmem] * 3,
-        out_specs=[vmem] * 2,
+        out_specs=[vmem] * 3,
         scratch_shapes=[
             pltpu.VMEM((tok, cols), jnp.float32),
-            pltpu.SemaphoreType.DMA((2, groups)),
-            pltpu.SemaphoreType.DMA((groups,)),
+            pltpu.SemaphoreType.DMA((2, groups, 2)),
+            pltpu.SemaphoreType.DMA((groups, 2)),
             pltpu.SemaphoreType.DMA((groups - 1, 2, seqs - 1)),
             pltpu.SemaphoreType.DMA((groups - 1, 2, seqs - 1)),
+            pltpu.SemaphoreType.DMA((groups - 1,)),
+            pltpu.SemaphoreType.DMA((groups - 1,)),
         ],
         compiler_params=pltpu.CompilerParams(has_side_effects=True),
         name="project",
@@ -489,13 +514,12 @@
     tok = hidden.shape[0]
     groups = lax.axis_size("fsdp")
     reach = groups // 2
-    weights, kv = project(hidden, kv_blocks, kv_scale)
+    weights, kv, columns = project(hidden, kv_blocks, kv_scale)
     pieces = []
     for offset in range(reach, 0, -1):
         pieces.append(shifted(kv, ("seq", "fsdp"), offset))
     window = jnp.concatenate(pieces + [kv], axis=0)
-    window, later = lax.optimization_barrier((window, hidden))
-    columns = lax.all_to_all(later, "fsdp", split_axis=1, concat_axis=0, tiled=True)
+    columns = columns.reshape(groups * tok, columns.shape[2])
     attn_out, grad_queries, dwin = attend(queries, window, grad_out, reach)
     back = dwin[: reach * tok].astype(jnp.bfloat16)
     own = dwin[reach * tok :]

time: 289 us -> 319 us (1.10)
  Pallas kernels: 224 us -> 276 us
  waiting for transfers between devices: 35 us -> 13.9 us
    pallas_call x1, Pallas kernels: 88 us -> 133 us  [project(): pl.pallas_call(functools.partial(project_kernel, seqs, groups), out_shape...]
    all_to_all x1 -> x0, waiting for transfers between devices: 19.5 us -> none  [body(): lax.all_to_all(later, 'fsdp', split_axis=1, concat_axis=0, tiled=True)]
    ppermute x2, starting transfers between devices: 5.07 us -> 13.6 us  [shifted(): return lax.ppermute(block, axis, route)]
    all_to_all x1 -> x0, starting transfers between devices: 6.96 us -> none  [body(): lax.all_to_all(later, 'fsdp', split_axis=1, concat_axis=0, tiled=True)]
    pallas_call x1, Pallas kernels: 113 us -> 119 us  [finish(): pl.pallas_call(functools.partial(finish_kernel, seqs, groups, reach), out...]
  transfers between devices with their start and end apart: 3 -> 2, of which waited for: 3 -> 2; matrix products, arithmetic and copies ran while one was open for 1% -> 0% of each run, Pallas kernels for 8% -> 0%
where the time goes in v3:
time: 319 us; the launch traced here: 318 us
  Pallas kernels  276 us (87%)
  waiting for transfers between devices  13.9 us (4%)
  starting transfers between devices  13.6 us (4%)
  other arithmetic  8.66 us (3%)
  local copies, waits for them, and re-layouts  5.94 us (2%)
    pallas_call x1, Pallas kernels, project(): pl.pallas_call(functools.partial(project_kernel, seqs, groups), out_shape...  133 us
    pallas_call x1, Pallas kernels, finish(): pl.pallas_call(functools.partial(finish_kernel, seqs, groups, reach), out...  119 us
    pallas_call x1, Pallas kernels, attend(): pl.pallas_call(functools.partial(attend_kernel, reach), grid=(heads,), in...  23.1 us
    ppermute x2, waiting for transfers between devices, shifted(): return lax.ppermute(block, axis, route)  13.9 us
    ppermute x2, starting transfers between devices, shifted(): return lax.ppermute(block, axis, route)  13.6 us
    convert_element_type x1, other arithmetic, body(): weight_grad.astype(jnp.float32)  6.78 us
  transfers between devices with their start and end apart: 2, of which 2 were waited for; matrix products, arithmetic and copies ran while one was open for 0% of the time, Pallas kernels for 0%

profile of v3, /device:TPU:27, one launch (start us, length us, event | category | flops | bytes accessed | tf_op | source)
XLA Modules:
  0.0 318.4 jit_solution(15883112803328399116)
XLA Ops:
  0.6 0.8 copy.9
  1.4 0.1 broadcast_in_dim.3
  1.5 0.7 copy.12
  2.1 133.2 %project.1 = (bf16[8192,1024]{1,0:T(8,128)(2,1)}, bf16[128,1024]{1,0:T(8,128)(2,1)}, bf16[4,128,2048]{2,1,0:T(8,128)(2,1)}) custom-call(bf16[128,8192]{1,0:T(8,128)(2,1)} %hid_ref.1, bf16[2048,1024]{1,0:T(8,128)(2,1)} %blk_ref.1, f32[16,1024]{1,0:T(8,128)} %bitcast.6), custom_call_target="tpu_custom_call" | custom-call | tf_op jit(solution)/shard_map/project/pallas_call | solution.py:251
  135.3 11.7 %collective-permute-start.1 = (bf16[128,1024]{1,0:T(8,128)(2,1)}, bf16[128,1024]{1,0:T(8,128)(2,1)S(1)}, u32[]{:S(2)}, u32[]{:S(2)}) collective-permute-start(bf16[128,1024]{1,0:T(8,128)(2,1)} %get-tuple-element.13), channel_id=1, source_target_pairs={{0,1},{1,2},{2,3},{3,4},{4,5},{5,6},{6,7},{7,8},{8,9},{9,10},{10,1... | collective-permute-start | bytes 786440 | tf_op jit(solution)/shard_map/ppermute | solution.py:22
  147.0 1.9 collective-permute-start
  148.9 2.6 collective-permute-done.1
  151.6 11.3 %collective-permute-done = bf16[128,1024]{1,0:T(8,128)(2,1)S(1)} collective-permute-done((bf16[128,1024]{1,0:T(8,128)(2,1)}, bf16[128,1024]{1,0:T(8,128)(2,1)S(1)}, u32[]{:S(2)}, u32[]{:S(2)}) %collective-permute-start) | collective-permute-done | bytes 262176 | tf_op jit(solution)/shard_map/ppermute | solution.py:22
  162.8 1.9 pad_maximum_fusion.k_ref.v_ref
  164.7 23.1 %attend.1 = (bf16[128,4096]{1,0:T(8,128)(2,1)}, bf16[128,4096]{1,0:T(8,128)(2,1)}, f32[384,512]{1,0:T(8,128)}, f32[384,512]{1,0:T(8,128)}) custom-call(bf16[128,4096]{1,0:T(8,128)(2,1)} %q_ref.1, bf16[128,4096]{1,0:T(8,128)(2,1)} %g_ref.1, bf16[384,1024]{1,0:T(8,128)(2,1)} %pad_maximum_fusion.k_ref.v_ref, bf16[384,1024]{1,0:T(8,128)(2,1)} %pad_maximum_fusion.k_ref.v_ref), custom_call_target="tpu_custom_call" | custom-call | flops 2415919104 | bytes 4194304 | tf_op jit(solution)/shard_map/attend/pallas_call | solution.py:70
  187.8 0.0 copy-start.1
  187.8 1.3 constant_dynamic-update-slice_fusion.1
  189.1 0.1 copy-done.1
  189.2 0.1 constant_dynamic-update-slice_fusion
  189.3 0.8 slice.10.own_ref
  190.1 0.9 slice.12.back_ref
  191.0 119.3 %finish.1 = (bf16[128,8192]{1,0:T(8,128)(2,1)}, bf16[2048,1024]{1,0:T(8,128)(2,1)}) custom-call(bf16[256,1024]{1,0:T(8,128)(2,1)} %slice.12.back_ref, f32[128,1024]{1,0:T(8,128)} %slice.10.own_ref, bf16[8192,1024]{1,0:T(8,128)(2,1)} %get-tuple-element.18.w_ref, bf16[512,2048]{1,0:T(8,128)(2,1)} %bitcast.5), custom_call_target="tpu_custom_call" | custom-call | tf_op jit(solution)/shard_map/finish/pallas_call | solution.py:484
  310.3 0.0 copy-start
  310.3 6.8 %convert_element_type.4 = f32[2048,1024]{1,0:T(8,128)} convert(bf16[2048,1024]{1,0:T(8,128)(2,1)} %get-tuple-element.21) | non-fusion elementwise | flops 2097152 | bytes 12582912 | tf_op jit(solution)/shard_map/convert_element_type | solution.py:527
  317.1 0.0 copy-done
  317.1 1.3 copy.15
Async XLA Ops:
  135.3 16.3 %collective-permute-start.1 = (bf16[128,1024]{1,0:T(8,128)(2,1)}, bf16[128,1024]{1,0:T(8,128)(2,1)S(1)}, u32[]{:S(2)}, u32[]{:S(2)}) collective-permute-start(bf16[128,1024]{1,0:T(8,128)(2,1)} %get-tuple-element.13), channel_id=1, source_target_pairs={{0,1},{1,2},{2,3},{3,4},{4,5},{5,6},{6,7},{7,8},{8,9},{9,10},{10,1... | collective-permute-start | bytes 786440 | tf_op jit(solution)/shard_map/ppermute | solution.py:22
  147.0 15.8 %collective-permute-start = (bf16[128,1024]{1,0:T(8,128)(2,1)}, bf16[128,1024]{1,0:T(8,128)(2,1)S(1)}, u32[]{:S(2)}, u32[]{:S(2)}) collective-permute-start(bf16[128,1024]{1,0:T(8,128)(2,1)} %get-tuple-element.13), channel_id=1, source_target_pairs={{0,2},{1,3},{2,4},{3,5},{4,6},{5,7},{6,8},{7,9},{8,10},{9,11},{10,... | collective-permute-start | bytes 786440 | tf_op jit(solution)/shard_map/ppermute | solution.py:22
  187.8 1.4 copy-start.1
  310.3 6.8 %copy-start = (bf16[128,8192]{1,0:T(8,128)(2,1)S(1)}, bf16[128,8192]{1,0:T(8,128)(2,1)}, u32[]{:S(2)}) copy-start(bf16[128,8192]{1,0:T(8,128)(2,1)} %get-tuple-element.28) | copy-start | bytes 6291460

commit v4 on v2

--- a/solution.py
+++ b/solution.py
@@ -95,7 +95,7 @@
     return (list(range(1, bits)) + [0], list(range(bits - 1, 0, -1)) + [0])
 
 
-def project_kernel(seqs, groups, hid_ref, blk_ref, sc_ref, w_ref, kv_ref, acc, zsend, zrecv, qsend, qrecv):
+def project_kernel(seqs, groups, hid_ref, blk_ref, sc_ref, out_ref, kv_ref, col_ref, w_ref, acc, zsend, zrecv, qsend, qrecv, csend, crecv, wsem):
     s = lax.axis_index("seq")
     z = lax.axis_index("fsdp")
     rows = blk_ref.shape[0]
@@ -162,7 +162,23 @@
     def _():
         line_copy(z, 0).start()
 
+    def column_copy(gap, incoming):
+        other = (z - gap + groups) % groups if incoming else (z + gap) % groups
+        part = pl.multiple_of(other * rows, 128)
+        return pltpu.make_async_remote_copy(
+            src_ref=hid_ref.at[:, pl.ds(part, rows)],
+            dst_ref=col_ref.at[other if incoming else z],
+            send_sem=csend.at[gap - 1],
+            recv_sem=crecv.at[gap - 1],
+            device_id=(s, other),
+            device_id_type=pl.DeviceIdType.MESH,
+        )
+
     acc[...] = jnp.zeros_like(acc)
+
+    def store_copy(turn, shard):
+        part = pl.ds(pl.multiple_of(shard * rows, 16), rows)
+        return pltpu.make_async_copy(w_ref.at[part, :], out_ref.at[part, :], wsem.at[turn])
 
     def multiply(shard):
         def part(i, carry):
@@ -175,6 +191,8 @@
         lax.fori_loop(0, rows // chunk, part, 0)
 
     multiply(z)
+    store_copy(groups - 1, z).start()
+    col_ref[z] = hid_ref[:, pl.ds(pl.multiple_of(z * rows, 128), rows)]
     for tick in range(groups - 1 + bits):
         for stage in range(bits, -1, -1):
             turn = tick - stage
@@ -201,7 +219,17 @@
                         cube_copy(turn, shard, order, stage, which, False).start()
             else:
                 multiply(shard)
+                store_copy(turn, shard).start()
+        if tick == groups - 2:
+            for gap in range(1, groups):
+                column_copy(gap, False).start()
     kv_ref[...] = acc[...].astype(jnp.bfloat16)
+    for turn in range(groups - 1):
+        store_copy(turn, shards[turn]).wait()
+    store_copy(groups - 1, z).wait()
+    for gap in range(1, groups):
+        column_copy(gap, True).wait_recv()
+        column_copy(gap, False).wait_send()
     for shard in range(groups):
 
         @pl.when((shard <= z) & (z < groups - 1))
@@ -231,15 +259,20 @@
         out_shape=[
             jax.ShapeDtypeStruct((width, cols), jnp.bfloat16),
             jax.ShapeDtypeStruct((tok, cols), jnp.bfloat16),
+            jax.ShapeDtypeStruct((groups, tok, kv_blocks.shape[0]), jnp.bfloat16),
         ],
         in_specs=[vmem] * 3,
-        out_specs=[vmem] * 2,
+        out_specs=[pl.BlockSpec(memory_space=pl.ANY), vmem, vmem],
         scratch_shapes=[
+            pltpu.VMEM((width, cols), jnp.bfloat16),
             pltpu.VMEM((tok, cols), jnp.float32),
             pltpu.SemaphoreType.DMA((2, groups)),
             pltpu.SemaphoreType.DMA((groups,)),
             pltpu.SemaphoreType.DMA((groups - 1, 2, seqs - 1)),
             pltpu.SemaphoreType.DMA((groups - 1, 2, seqs - 1)),
+            pltpu.SemaphoreType.DMA((groups - 1,)),
+            pltpu.SemaphoreType.DMA((groups - 1,)),
+            pltpu.SemaphoreType.DMA((groups,)),
         ],
         compiler_params=pltpu.CompilerParams(has_side_effects=True),
         name="project",
@@ -247,8 +280,8 @@
 
 
 def finish_kernel(
-    seqs, groups, reach, back_ref, own_ref, w_ref, col_ref, gh_ref, wg_ref,
-    ret, every, inside, acc, sends, recvs, hsend, hrecv, gsend, grecv, rsend, rrecv, asend, arecv,
+    seqs, groups, reach, back_ref, own_ref, in_ref, col_ref, gh_ref, wg_ref,
+    w_ref, wsem, ret, every, inside, acc, sends, recvs, hsend, hrecv, gsend, grecv, rsend, rrecv, asend, arecv,
 ):
     s = lax.axis_index("seq")
     z = lax.axis_index("fsdp")
@@ -258,6 +291,8 @@
     rows = col_ref.shape[1]
     bits = seqs.bit_length() - 1
     mesh_id = pl.DeviceIdType.MESH
+    load = pltpu.make_async_copy(in_ref, w_ref, wsem)
+    load.start()
 
     def halo_copy(offset, incoming):
         other = linear + offset if incoming else linear - offset
@@ -310,6 +345,7 @@
     for gap in range(1, groups):
         gather_copy(gap, False).start()
 
+    load.wait()
     wide = 512
 
     def spread(i, carry):
@@ -462,9 +498,11 @@
             jax.ShapeDtypeStruct((tok, weights.shape[0]), jnp.bfloat16),
             jax.ShapeDtypeStruct((rows, cols), jnp.bfloat16),
         ],
-        in_specs=[vmem] * 4,
+        in_specs=[vmem, vmem, pl.BlockSpec(memory_space=pl.ANY), vmem],
         out_specs=[vmem] * 2,
         scratch_shapes=[
+            pltpu.VMEM(weights.shape, jnp.bfloat16),
+            dma(()),
             pltpu.VMEM((reach, tok, cols), jnp.bfloat16),
             pltpu.VMEM((groups, tok, cols), jnp.bfloat16),
             pltpu.VMEM((tok, cols), jnp.bfloat16),
@@ -489,13 +527,12 @@
     tok = hidden.shape[0]
     groups = lax.axis_size("fsdp")
     reach = groups // 2
-    weights, kv = project(hidden, kv_blocks, kv_scale)
+    weights, kv, columns = project(hidden, kv_blocks, kv_scale)
     pieces = []
     for offset in range(reach, 0, -1):
         pieces.append(shifted(kv, ("seq", "fsdp"), offset))
     window = jnp.concatenate(pieces + [kv], axis=0)
-    window, later = lax.optimization_barrier((window, hidden))
-    columns = lax.all_to_all(later, "fsdp", split_axis=1, concat_axis=0, tiled=True)
+    columns = columns.reshape(groups * tok, columns.shape[2])
     attn_out, grad_queries, dwin = attend(queries, window, grad_out, reach)
     back = dwin[: reach * tok].astype(jnp.bfloat16)
     own = dwin[reach * tok :]

time: 289 us -> 280 us (0.969)
  waiting for transfers between devices: 35 us -> 12.9 us
  Pallas kernels: 224 us -> 244 us
  starting transfers between devices: 12 us -> 7.28 us
    pallas_call x1, Pallas kernels: 88 us -> 110 us  [project(): pl.pallas_call(functools.partial(project_kernel, seqs, groups), out_shape...]
    all_to_all x1 -> x0, waiting for transfers between devices: 19.5 us -> none  [body(): lax.all_to_all(later, 'fsdp', split_axis=1, concat_axis=0, tiled=True)]
    all_to_all x1 -> x0, starting transfers between devices: 6.96 us -> none  [body(): lax.all_to_all(later, 'fsdp', split_axis=1, concat_axis=0, tiled=True)]
  transfers between devices with their start and end apart: 3 -> 2, of which waited for: 3 -> 2; matrix products, arithmetic and copies ran while one was open for 1% -> 0% of each run, Pallas kernels for 8% -> 0%
where the time goes in v4:
time: 280 us
  Pallas kernels  244 us (87%)
  waiting for transfers between devices  12.9 us (5%)
  other arithmetic  8.66 us (3%)
  starting transfers between devices  7.28 us (3%)
  local copies, waits for them, and re-layouts  5.94 us (2%)
    pallas_call x1, Pallas kernels, finish(): pl.pallas_call(functools.partial(finish_kernel, seqs, groups, reach), out...  112 us
    pallas_call x1, Pallas kernels, project(): pl.pallas_call(functools.partial(project_kernel, seqs, groups), out_shape...  110 us
    pallas_call x1, Pallas kernels, attend(): pl.pallas_call(functools.partial(attend_kernel, reach), grid=(heads,), in...  23.1 us
    ppermute x2, waiting for transfers between devices, shifted(): return lax.ppermute(block, axis, route)  12.9 us
    ppermute x2, starting transfers between devices, shifted(): return lax.ppermute(block, axis, route)  7.28 us
    convert_element_type x1, other arithmetic, body(): weight_grad.astype(jnp.float32)  6.78 us
  transfers between devices with their start and end apart: 2, of which 2 were waited for; matrix products, arithmetic and copies ran while one was open for 0% of the time, Pallas kernels for 0%

profile of v4, /device:TPU:27, one launch (start us, length us, event | category | flops | bytes accessed | tf_op | source)
XLA Modules:
  0.0 280.0 jit_solution(3531796842133606804)
XLA Ops:
  0.6 0.8 copy.9
  1.4 0.1 broadcast_in_dim.3
  1.5 0.7 copy.12
  2.1 109.6 %project.1 = (bf16[8192,1024]{1,0:T(8,128)(2,1)}, bf16[128,1024]{1,0:T(8,128)(2,1)}, bf16[4,128,2048]{2,1,0:T(8,128)(2,1)}) custom-call(bf16[128,8192]{1,0:T(8,128)(2,1)} %hid_ref.1, bf16[2048,1024]{1,0:T(8,128)(2,1)} %blk_ref.1, f32[16,1024]{1,0:T(8,128)} %bitcast.6), custom_call_target="tpu_custom_call" | custom-call | tf_op jit(solution)/shard_map/project/pallas_call | solution.py:257
  111.7 5.4 %collective-permute-start.1 = (bf16[128,1024]{1,0:T(8,128)(2,1)}, bf16[128,1024]{1,0:T(8,128)(2,1)S(1)}, u32[]{:S(2)}, u32[]{:S(2)}) collective-permute-start(bf16[128,1024]{1,0:T(8,128)(2,1)} %get-tuple-element.13), channel_id=1, source_target_pairs={{0,1},{1,2},{2,3},{3,4},{4,5},{5,6},{6,7},{7,8},{8,9},{9,10},{10,1... | collective-permute-start | bytes 786440 | tf_op jit(solution)/shard_map/ppermute | solution.py:22
  117.0 1.9 collective-permute-start
  119.0 4.3 %collective-permute-done.1 = bf16[128,1024]{1,0:T(8,128)(2,1)S(1)} collective-permute-done((bf16[128,1024]{1,0:T(8,128)(2,1)}, bf16[128,1024]{1,0:T(8,128)(2,1)S(1)}, u32[]{:S(2)}, u32[]{:S(2)}) %collective-permute-start.1) | collective-permute-done | bytes 262176 | tf_op jit(solution)/shard_map/ppermute | solution.py:22
  123.3 8.6 %collective-permute-done = bf16[128,1024]{1,0:T(8,128)(2,1)S(1)} collective-permute-done((bf16[128,1024]{1,0:T(8,128)(2,1)}, bf16[128,1024]{1,0:T(8,128)(2,1)S(1)}, u32[]{:S(2)}, u32[]{:S(2)}) %collective-permute-start) | collective-permute-done | bytes 262176 | tf_op jit(solution)/shard_map/ppermute | solution.py:22
  131.9 1.9 pad_maximum_fusion.k_ref.v_ref
  133.8 23.1 %attend.1 = (bf16[128,4096]{1,0:T(8,128)(2,1)}, bf16[128,4096]{1,0:T(8,128)(2,1)}, f32[384,512]{1,0:T(8,128)}, f32[384,512]{1,0:T(8,128)}) custom-call(bf16[128,4096]{1,0:T(8,128)(2,1)} %q_ref.1, bf16[128,4096]{1,0:T(8,128)(2,1)} %g_ref.1, bf16[384,1024]{1,0:T(8,128)(2,1)} %pad_maximum_fusion.k_ref.v_ref, bf16[384,1024]{1,0:T(8,128)(2,1)} %pad_maximum_fusion.k_ref.v_ref), custom_call_target="tpu_custom_call" | custom-call | flops 2415919104 | bytes 4194304 | tf_op jit(solution)/shard_map/attend/pallas_call | solution.py:70
  156.9 0.0 copy-start.1
  156.9 1.3 constant_dynamic-update-slice_fusion.1
  158.2 0.1 copy-done.1
  158.3 0.1 constant_dynamic-update-slice_fusion
  158.3 0.8 slice.10.own_ref
  159.2 0.9 slice.12.back_ref
  160.0 111.8 %finish.1 = (bf16[128,8192]{1,0:T(8,128)(2,1)}, bf16[2048,1024]{1,0:T(8,128)(2,1)}) custom-call(bf16[256,1024]{1,0:T(8,128)(2,1)} %slice.12.back_ref, f32[128,1024]{1,0:T(8,128)} %slice.10.own_ref, bf16[8192,1024]{1,0:T(8,128)(2,1)} %get-tuple-element.18.in_ref, bf16[512,2048]{1,0:T(8,128)(2,1)} %bitcast.5), custom_call_target="tpu_custom_call" | custom-call | tf_op jit(solution)/shard_map/finish/pallas_call | solution.py:495
  271.8 0.0 copy-start
  271.9 6.8 %convert_element_type.4 = f32[2048,1024]{1,0:T(8,128)} convert(bf16[2048,1024]{1,0:T(8,128)(2,1)} %get-tuple-element.21) | non-fusion elementwise | flops 2097152 | bytes 12582912 | tf_op jit(solution)/shard_map/convert_element_type | solution.py:540
  278.6 0.0 copy-done
  278.6 1.3 copy.15
Async XLA Ops:
  111.7 11.6 %collective-permute-start.1 = (bf16[128,1024]{1,0:T(8,128)(2,1)}, bf16[128,1024]{1,0:T(8,128)(2,1)S(1)}, u32[]{:S(2)}, u32[]{:S(2)}) collective-permute-start(bf16[128,1024]{1,0:T(8,128)(2,1)} %get-tuple-element.13), channel_id=1, source_target_pairs={{0,1},{1,2},{2,3},{3,4},{4,5},{5,6},{6,7},{7,8},{8,9},{9,10},{10,1... | collective-permute-start | bytes 786440 | tf_op jit(solution)/shard_map/ppermute | solution.py:22
  117.0 14.8 %collective-permute-start = (bf16[128,1024]{1,0:T(8,128)(2,1)}, bf16[128,1024]{1,0:T(8,128)(2,1)S(1)}, u32[]{:S(2)}, u32[]{:S(2)}) collective-permute-start(bf16[128,1024]{1,0:T(8,128)(2,1)} %get-tuple-element.13), channel_id=1, source_target_pairs={{0,2},{1,3},{2,4},{3,5},{4,6},{5,7},{6,8},{7,9},{8,10},{9,11},{10,... | collective-permute-start | bytes 786440 | tf_op jit(solution)/shard_map/ppermute | solution.py:22
  156.9 1.4 copy-start.1
  271.8 6.8 %copy-start = (bf16[128,8192]{1,0:T(8,128)(2,1)S(1)}, bf16[128,8192]{1,0:T(8,128)(2,1)}, u32[]{:S(2)}) copy-start(bf16[128,8192]{1,0:T(8,128)(2,1)} %get-tuple-element.28) | copy-start | bytes 6291460
